TPU v7x, 256 devices: a whole 4x4x8 slice. The times are simulated.
256 devices in a mesh: mem: 16 (over z, core), ma: 16 (over x, y).
Axes of the slice: x: 4, y: 4, z: 8, core: 2. Of those that a mesh axis runs over, the one named last changes fastest.
Arguments:
- ar_state: float32 [3, 64, 128, 2, 1280], P(None, 'mem', 'ma'), may hold values from -4 to 4
- forcing: float32 [3, 64, 128, 2, 1280], P(None, 'mem', 'ma'), may hold values from -6 to 6
- ar_decay: float32 [3], replicated, may hold values from 0.3 to 0.95
- amplitude: float32 [3, 1280], replicated, may hold values from 0.05 to 0.4
- wavenumber: int32 [128], replicated, may hold values from 0 to 1279, as said below
- tables: bfloat16 [128, 1280, 1280], P('ma', None, 'mem'), may hold values from -0.15625 to 0.15625
- tendencies: bfloat16 [64, 1280, 5120], P('mem', 'ma'), may hold values from -6 to 6
Outputs:
- perturbed: bfloat16 [64, 1280, 5120], P('mem', 'ma')
- new_state: float32 [3, 64, 128, 2, 1280], P(None, 'mem', 'ma')
Inputs may be any that keep to these rules, and one draw needn't show every extreme that they name: `wavenumber`: 128 distinct values.
All inputs are finite; a program needn't handle non-finite values.
Results may differ from a plain program's by a relative error of at most 0.0042.
Values may be sent and summed in bfloat16 or wider, within the bound.
No kernel may reach another device: no remote copies, remote signals or barrier semaphores. Data moves between devices by JAX's collectives and lax.ppermute only.
A program may use at most 64 MiB of HBM per device.

v0:
```python
import math

import jax
import jax.numpy as jnp
from jax import lax
from jax.sharding import PartitionSpec as P

clip_level = 0.9


def basis_table(wavenumber, lon_count):
    longitude = lax.broadcasted_iota(jnp.int32, (wavenumber.shape[0], lon_count), 1)
    phases = wavenumber[:, None] * longitude % lon_count
    angles = phases.astype(jnp.float32) * (2.0 * math.pi / lon_count)
    stacked = jnp.stack([jnp.cos(angles), -jnp.sin(angles)], axis=1)
    return stacked.reshape(2 * wavenumber.shape[0], lon_count).astype(jnp.bfloat16)


def per_device(ar_state, forcing, ar_decay, amplitude, wavenumber, tables, tendencies):
    local_waves = ar_state.shape[2]
    degree_count = ar_state.shape[4]
    owner_index = lax.axis_index("ma")
    own_waves = lax.dynamic_slice_in_dim(wavenumber, owner_index * local_waves, local_waves)
    degree_grid = lax.broadcasted_iota(jnp.int32, (local_waves, degree_count), 1)
    kept_mask = (degree_grid >= own_waves[:, None]).astype(jnp.float32)
    updated = (
        ar_decay[:, None, None, None, None] * ar_state + amplitude[:, None, None, None, :] * forcing
    )
    new_state = kept_mask[None, None, :, None, :] * updated
    coefficients = jnp.sum(new_state, axis=0).astype(jnp.bfloat16)
    everyone = lax.all_gather(coefficients, "mem", axis=0, tiled=True)
    product = jnp.einsum("bmcn,mnl->blmc", everyone, tables, preferred_element_type=jnp.float32)
    fourier = product.astype(jnp.bfloat16)
    banded = lax.all_to_all(
        lax.all_to_all(fourier, "mem", split_axis=0, concat_axis=1, tiled=True),
        "ma",
        split_axis=1,
        concat_axis=2,
        tiled=True,
    )
    member_count, lat_rows, window_size, reim_parts = banded.shape
    basis = basis_table(wavenumber, tendencies.shape[2])
    fourier_rows = banded.reshape(member_count * lat_rows, window_size * reim_parts)
    pattern = jnp.dot(fourier_rows, basis, preferred_element_type=jnp.float32) * (
        1.0 / math.sqrt(window_size)
    )
    pattern = jnp.clip(pattern, -clip_level, clip_level).reshape(tendencies.shape)
    perturbed = (tendencies.astype(jnp.float32) * (1.0 + pattern)).astype(jnp.bfloat16)
    return (perturbed, new_state)


def solution(mesh):
    return jax.shard_map(
        per_device,
        mesh=mesh,
        in_specs=(
            P(None, "mem", "ma", None, None),
            P(None, "mem", "ma", None, None),
            P(),
            P(),
            P(),
            P("ma", None, "mem"),
            P("mem", "ma", None),
        ),
        out_specs=(P("mem", "ma", None), P(None, "mem", "ma", None, None)),
        check_vma=False,
    )
```

profile of v0, /device:TPU:2, one launch (start us, length us, event | category | flops | bytes accessed | tf_op | source)
XLA Modules:
  0.0 130.5 jit_solution(6090136942241296516)
XLA Ops:
  7.2 0.0 copy-start
  7.2 0.0 all-gather.2.cloned.1.call-start
  7.2 0.8 dynamic_slice.3
  8.1 0.1 fusion.20
  8.1 3.5 %fusion.21 = (bf16[4,8,2,1280]{3,2,1,0:T(2,128)(2,1)S(1)}, f32[3,4,8,2,1280]{4,3,2,1,0:T(2,128)}) fusion(f32[3,4,8,2,1280]{4,3,2,1,0:T(2,128)} %param.8, f32[3,1280]{1,0:T(4,128)} %param.10, f32[3,4,8,2,1280]{4,3,2,1,0:T(2,128)} %param.7, f32[3]{0:T(128)} %param.9, f32[8,1280]{1,0:T(8,128)S(1)} %fusion.20), kind=kLoop, calls=%fused_computation.23 | loop fusion | flops 1146880 | bytes 3169292 | tf_op jit(solution)/shard_map/reduce_sum | solution.py:30
  11.6 0.7 copy.23
  12.3 0.0 all-gather.2.cloned.1.call-update
  12.3 0.0 copy-start.2
  12.3 43.2 %all-gather.2.cloned.1.call-done = bf16[64,8,2,1280]{3,1,2,0:T(8,128)(2,1)} async-done(((bf16[4,8,2,1280]{3,1,2,0:T(8,128)(2,1)}), bf16[64,8,2,1280]{3,1,2,0:T(8,128)(2,1)}) %all-gather.2.cloned.1.call-update) | async-done | bytes 2621456 | tf_op jit(solution)/shard_map/all_gather | solution.py:31
  55.5 0.0 copy-done
  55.5 2.7 %fusion.15 = bf16[64,80,8,2]{1,0,3,2:T(8,128)(2,1)S(1)} fusion(bf16[8,1280,80]{1,2,0:T(8,128)(2,1)S(1)} %copy-done, bf16[64,8,2,1280]{3,1,2,0:T(8,128)(2,1)} %all-gather.2.cloned.1.call-done), kind=kOutput, calls=%fused_computation.18 | convolution fusion | flops 209797120 | bytes 4423680 | tf_op jit(solution)/shard_map/bmcn,mnl->blmc/dot_general | solution.py:32
  58.2 1.0 copy.25
  59.2 4.4 %all-to-all-start = ((bf16[64,80,8,2]{1,3,2,0:T(2,128)(2,1)}), bf16[64,80,8,2]{1,3,2,0:T(2,128)(2,1)S(1)}, u32[]{:S(2)}, u32[]{:S(2)}) async-start(bf16[64,80,8,2]{1,3,2,0:T(2,128)(2,1)} %copy.25), calls=%async_computation | async-start | bytes 524288 | tf_op jit(solution)/shard_map/all_to_all | solution.py:35
  63.6 0.0 copy-done.2
  63.6 12.1 %cosine_convert_fusion = (bf16[128,1,5120]{2,0,1:T(8,128)(2,1)S(1)}, bf16[128,1,5120]{2,0,1:T(8,128)(2,1)}) fusion(s32[128]{0:T(128)S(1)} %copy-done.2), kind=kLoop, calls=%fused_computation.11 | loop fusion | flops 7864320 | bytes 2621952 | tf_op jit(solution)/shard_map/convert
  75.7 0.0 all-to-all-done
  75.7 0.2 copy.39
  75.8 4.0 %copy.31 = bf16[4,16,80,8,2]{3,4,0,2,1:T(2,128)(2,1)} copy(bf16[4,16,80,8,2]{2,1,3,4,0:T(8,128)(2,1)S(1)} %bitcast.30) | data formatting | bytes 327680 | tf_op jit(solution)/shard_map/all_to_all | solution.py:35
  79.8 8.6 %reshape.114 = bf16[16,2,2560]{2,1,0:T(2,128)(2,1)} reshape(bf16[1280,4,2,8]{3,2,1,0:T(2,128)(2,1)} %bitcast.26) | data formatting | bytes 327680
  88.4 7.3 %all-to-all-start.1 = ((bf16[16,2,2560]{2,1,0:T(2,128)(2,1)}), bf16[16,2,2560]{2,1,0:T(2,128)(2,1)S(1)}, u32[]{:S(2)}, u32[]{:S(2)}) async-start(bf16[16,2,2560]{2,1,0:T(2,128)(2,1)} %reshape.114), calls=%async_computation.1 | async-start | bytes 327680 | tf_op jit(solution)/shard_map/all_to_all | solution.py:34
  95.7 1.6 %pad_maximum_fusion = bf16[128,2,5120]{2,0,1:T(8,128)(2,1)S(1)} fusion(bf16[128,1,5120]{2,0,1:T(8,128)(2,1)} %get-tuple-element.5, bf16[128,1,5120]{2,0,1:T(8,128)(2,1)S(1)} %get-tuple-element.4), kind=kLoop, calls=%fused_computation.7 | loop fusion | flops 1310720 | bytes 5242880 | tf_op jit(solution)/shard_map/stack | solution.py:15
  97.3 4.2 %copy.29 = bf16[128,2,5120]{2,1,0:T(2,128)(2,1)} copy(bf16[128,2,5120]{2,0,1:T(8,128)(2,1)S(1)} %pad_maximum_fusion) | data formatting | bytes 5242880 | tf_op jit(solution)/shard_map/stack | solution.py:15
  101.5 6.5 %convert_element_type.52 = bf16[256,5120]{1,0:T(8,128)(2,1)} reshape(bf16[128,2,5120]{2,1,0:T(2,128)(2,1)} %copy.29) | data formatting | bytes 5242880 | tf_op jit(solution)/shard_map/convert_element_type | solution.py:16
  107.9 0.0 all-to-all-done.1
  107.9 4.1 %reshape.115 = bf16[1280,4,2,8]{3,2,1,0:T(2,128)(2,1)} reshape(bf16[16,2,2560]{2,1,0:T(2,128)(2,1)S(1)} %all-to-all-done.1) | data formatting | bytes 327680
  112.1 5.2 %copy.28 = bf16[4,16,80,8,2]{2,0,4,3,1:T(4,128)(2,1)S(1)} copy(bf16[4,16,80,8,2]{3,4,0,2,1:T(2,128)(2,1)} %bitcast.27) | data formatting | bytes 327680 | tf_op jit(solution)/shard_map/all_to_all | solution.py:34
  117.2 0.2 reshape.112
  117.4 0.0 copy-start.1
  117.5 3.4 %fusion.1 = f32[320,5120]{1,0:T(8,128)S(1)} fusion(bf16[320,256]{0,1:T(8,128)(2,1)S(1)} %reshape.112, bf16[256,5120]{1,0:T(8,128)(2,1)} %convert_element_type.52), kind=kOutput, calls=%fused_computation.2 | convolution fusion | flops 843776000 | bytes 9338880 | tf_op jit(solution)/shard_map/dot_general | solution.py:44
  120.9 0.0 copy-done.1
  120.9 2.7 %multiply_convert_fusion = bf16[4,80,5120]{2,1,0:T(8,128)(2,1)} fusion(f32[4,80,5120]{2,1,0:T(8,128)S(1)} %bitcast.25, bf16[4,80,5120]{2,1,0:T(8,128)(2,1)S(1)} %copy-done.1), kind=kLoop, calls=%fused_computation.3 | loop fusion | flops 4915200 | bytes 13107200 | tf_op jit(solution)/shard_map/convert_element_type | solution.py:48
Async XLA Ops:
  7.2 48.3 %copy-start = (bf16[8,1280,80]{1,2,0:T(8,128)(2,1)S(1)}, bf16[8,1280,80]{1,2,0:T(8,128)(2,1)}, u32[]{:S(2)}) copy-start(bf16[8,1280,80]{1,2,0:T(8,128)(2,1)} %param.12) | copy-start | bytes 4915204
  7.2 48.3 %all-gather.2.cloned.1.call-start = ((), (), s32[]{:S(2)}) async-start(), calls=%async_computation.2 | async-start | bytes 2785280 | tf_op jit(solution)/shard_map/all_gather | solution.py:31
  12.3 51.3 %copy-start.2 = (s32[128]{0:T(128)S(1)}, s32[128]{0:T(128)}, u32[]{:S(2)}) copy-start(s32[128]{0:T(128)} %param.11) | copy-start | bytes 1540
  59.2 16.5 %all-to-all-start = ((bf16[64,80,8,2]{1,3,2,0:T(2,128)(2,1)}), bf16[64,80,8,2]{1,3,2,0:T(2,128)(2,1)S(1)}, u32[]{:S(2)}, u32[]{:S(2)}) async-start(bf16[64,80,8,2]{1,3,2,0:T(2,128)(2,1)} %copy.25), calls=%async_computation | async-start | bytes 524288 | tf_op jit(solution)/shard_map/all_to_all | solution.py:35
  88.4 19.5 %all-to-all-start.1 = ((bf16[16,2,2560]{2,1,0:T(2,128)(2,1)}), bf16[16,2,2560]{2,1,0:T(2,128)(2,1)S(1)}, u32[]{:S(2)}, u32[]{:S(2)}) async-start(bf16[16,2,2560]{2,1,0:T(2,128)(2,1)} %reshape.114), calls=%async_computation.1 | async-start | bytes 327680 | tf_op jit(solution)/shard_map/all_to_all | solution.py:34
  117.4 3.4 %copy-start.1 = (bf16[4,80,5120]{2,1,0:T(8,128)(2,1)S(1)}, bf16[4,80,5120]{2,1,0:T(8,128)(2,1)}, u32[]{:S(2)}) copy-start(bf16[4,80,5120]{2,1,0:T(8,128)(2,1)} %param.13) | copy-start | bytes 9830404
Sparse Core Ops, SparseCore 0:
  12.4 43.0 all-gather.1
where the time goes:
time: 132 us; the launch traced here: 130 us
  waiting for transfers between devices  43.2 us (33%)
  local copies, waits for them, and re-layouts  35.5 us (27%)
  other arithmetic  19.9 us (15%)
  between operations  14.1 us (11%)
  starting transfers between devices  11.7 us (9%)
  matrix products  6.1 us (5%)
    all_gather x1, waiting for transfers between devices, per_device(): everyone = lax.all_gather(coefficients, 'mem', axis=0, tiled=True)  43.2 us
    unnamed x8, local copies, waits for them, and re-layouts  12.8 us
    another operation x1, other arithmetic  12.1 us
    all_to_all x1, starting transfers between devices, per_device(): lax.all_to_all(lax.all_to_all(fourier, 'mem', split_axis=0, concat_axis=1...  7.27 us
    convert_element_type x1, local copies, waits for them, and re-layouts, basis_table(): stacked.reshape(2 * wavenumber.shape[0], lon_count).astype(jnp.bfloat16)  6.47 us
    all_to_all x1, local copies, waits for them, and re-layouts, per_device(): lax.all_to_all(lax.all_to_all(fourier, 'mem', split_axis=0, concat_axis=1...  5.18 us
    all_to_all x1, starting transfers between devices, per_device(): lax.all_to_all(fourier, 'mem', split_axis=0, concat_axis=1, tiled=True)  4.39 us
    another operation x1, local copies, waits for them, and re-layouts, basis_table(): stacked = jnp.stack([jnp.cos(angles), -jnp.sin(angles)], axis=1)  4.19 us
  transfers between devices with their start and end apart: 3, of which 1 were waited for; matrix products, arithmetic and copies ran while one was open for 19% of the time, Pallas kernels for 0%

commit v1 on v0

v1 whole, which is shorter than its diff:
```python
import functools
import math

import jax
import jax.numpy as jnp
from jax import lax
from jax.experimental import pallas as pl
from jax.experimental.pallas import tpu as pltpu
from jax.sharding import PartitionSpec as P

clip_level = 0.9
cores = 2
contract_last = (((1,), (1,)), ((), ()))
contract_first = (((0,), (0,)), ((), ()))
megabyte = 1 << 20


def ring_shift(mesh_size, shift):
    chips = mesh_size // cores
    return [
        (z * cores + c, ((z + shift) % chips) * cores + c) for z in range(chips) for c in range(cores)
    ]


def core_swap(mesh_size):
    return [(m, m ^ 1) for m in range(mesh_size)]


def update_kernel(wave_ref, decay_ref, amplitude_ref, state_ref, forcing_ref, new_ref, coef_ref):
    step = pl.program_id(0)
    scales, members, waves, parts, degrees = state_ref.shape
    total_waves = waves * pl.num_programs(0)
    degree = lax.broadcasted_iota(jnp.int32, (parts, degrees), 1)
    for j in range(waves):
        first = wave_ref[lax.axis_index("ma") * total_waves + step * waves + j]
        kept = degree >= first
        rows = []
        for b in range(members):
            total = None
            for s in range(scales):
                value = (
                    decay_ref[s] * state_ref[s, b, j]
                    + amplitude_ref[s : s + 1, :] * forcing_ref[s, b, j]
                )
                value = jnp.where(kept, value, 0.0)
                new_ref[s, b, j] = value
                total = value if total is None else total + value
            rows.append(total)
        coef_ref[j] = jnp.concatenate(rows, axis=0).astype(jnp.bfloat16)


def update(wavenumber, ar_decay, amplitude, ar_state, forcing):
    scales, members, waves, parts, degrees = ar_state.shape
    per_step = 2
    block = pl.BlockSpec(
        (scales, members, per_step, parts, degrees), lambda i: (0, 0, i, 0, 0)
    )
    return pl.pallas_call(
        update_kernel,
        grid=(waves // per_step,),
        in_specs=[
            pl.BlockSpec(memory_space=pltpu.SMEM),
            pl.BlockSpec(memory_space=pltpu.SMEM),
            pl.BlockSpec((scales, degrees), lambda i: (0, 0)),
            block,
            block,
        ],
        out_specs=[
            block,
            pl.BlockSpec((per_step, members * parts, degrees), lambda i: (i, 0, 0)),
        ],
        out_shape=[
            jax.ShapeDtypeStruct(ar_state.shape, jnp.float32),
            jax.ShapeDtypeStruct((waves, members * parts, degrees), jnp.bfloat16),
        ],
        compiler_params=pltpu.CompilerParams(vmem_limit_bytes=16 * megabyte),
        name="update",
    )(wavenumber, ar_decay, amplitude, ar_state, forcing)


def legendre_kernel(layout, members, own_ref, other_ref, *refs):
    blocks = refs[: sum(layout)]
    outs = refs[sum(layout) : -1]
    stage = refs[-1]
    waves, lats, _ = own_ref.shape
    core = lax.axis_index("mem") % cores
    at = 0
    for count, out_ref in zip(layout, outs):
        pieces = blocks[at : at + count]
        at += count
        for j in range(waves):
            piece = pieces[j // (waves // count)]
            rows = piece[j % (waves // count)]
            for side, table_ref in enumerate((own_ref, other_ref)):
                product = lax.dot_general(
                    rows, table_ref[j], contract_last, preferred_element_type=jnp.float32
                )
                for b in range(members):
                    for c in range(2):
                        stage[side, c * waves + j, b * lats : (b + 1) * lats] = product[2 * b + c]
        out_ref[core] = stage[0].astype(jnp.bfloat16)
        out_ref[1 - core] = stage[1].astype(jnp.bfloat16)


def legendre(tables, blocks, members):
    waves, lats, degrees = tables[0].shape
    layout = tuple(len(b) for b in blocks)
    flat = [piece for b in blocks for piece in b]
    whole = pl.BlockSpec(memory_space=pltpu.VMEM)
    shape = (cores, 2 * waves, members * lats)
    return pl.pallas_call(
        functools.partial(legendre_kernel, layout, members),
        in_specs=[whole] * (2 + len(flat)),
        out_specs=[whole] * len(blocks),
        out_shape=[jax.ShapeDtypeStruct(shape, jnp.bfloat16)] * len(blocks),
        scratch_shapes=[pltpu.VMEM(shape, jnp.float32)],
        compiler_params=pltpu.CompilerParams(vmem_limit_bytes=16 * megabyte),
        cost_estimate=pl.CostEstimate(
            flops=len(blocks) * 1_000_000_000, bytes_accessed=4 * megabyte, transcendentals=0
        ),
        name="legendre",
    )(*tables, *flat)


def arrange_kernel(*refs):
    pieces, out_ref = refs[:-1], refs[-1]
    chips = len(pieces)
    here = lax.axis_index("mem") // cores
    for d, piece in enumerate(pieces):
        there = lax.rem(here + d, chips)
        for c in range(cores):
            out_ref[there * cores + c] = piece[c]


def arrange(pieces):
    whole = pl.BlockSpec(memory_space=pltpu.VMEM)
    _, rows, columns = pieces[0].shape
    return pl.pallas_call(
        arrange_kernel,
        in_specs=[whole] * len(pieces),
        out_specs=whole,
        out_shape=jax.ShapeDtypeStruct((len(pieces) * cores, rows, columns), jnp.bfloat16),
        compiler_params=pltpu.CompilerParams(vmem_limit_bytes=4 * megabyte),
        name="arrange",
    )(*pieces)


def basis_kernel(owners, wave_ref, out_ref):
    window, lanes = wave_ref.shape[0], 128
    lon_count = out_ref.shape[1]
    waves = window // owners
    tiles = lon_count // lanes
    wave = wave_ref[...]
    lane = lax.broadcasted_iota(jnp.int32, (window, lanes), 1)
    turn = 2.0 * math.pi / lon_count
    fine = (lax.rem(wave * lane, lon_count)).astype(jnp.float32) * turn
    coarse = (lax.rem(wave * lanes * lane, lon_count)).astype(jnp.float32) * turn
    cos_fine, sin_fine = jnp.cos(fine), jnp.sin(fine)
    cos_coarse, sin_coarse = jnp.cos(coarse), jnp.sin(coarse)
    for t in range(tiles):
        ca, sa = cos_coarse[:, t : t + 1], sin_coarse[:, t : t + 1]
        cosine = ca * cos_fine - sa * sin_fine
        minus_sine = -(sa * cos_fine + ca * sin_fine)
        for a in range(owners):
            rows = slice(a * waves, (a + 1) * waves)
            both = jnp.concatenate([cosine[rows], minus_sine[rows]], axis=0)
            out_ref[2 * a * waves : 2 * (a + 1) * waves, t * lanes : (t + 1) * lanes] = both.astype(
                jnp.bfloat16
            )


def basis_table(wavenumber, lon_count, owners):
    window = wavenumber.shape[0]
    return pl.pallas_call(
        functools.partial(basis_kernel, owners),
        in_specs=[pl.BlockSpec(memory_space=pltpu.VMEM)],
        out_specs=pl.BlockSpec(memory_space=pltpu.VMEM),
        out_shape=jax.ShapeDtypeStruct((2 * window, lon_count), jnp.bfloat16),
        compiler_params=pltpu.CompilerParams(vmem_limit_bytes=16 * megabyte),
        cost_estimate=pl.CostEstimate(
            flops=2_000_000_000, bytes_accessed=3 * megabyte, transcendentals=65536
        ),
        name="basis",
    )(wavenumber.reshape(window, 1))


def grid_kernel(scale, rows_ref, basis_ref, tend_ref, out_ref):
    pattern = lax.dot_general(
        rows_ref[...], basis_ref[...], contract_first, preferred_element_type=jnp.float32
    )
    pattern = jnp.clip(pattern * scale, -clip_level, clip_level)
    out_ref[...] = (tend_ref[...].astype(jnp.float32) * (1.0 + pattern)).astype(jnp.bfloat16)


def to_grid(rows, basis, tendencies, scale):
    members, lats, lons = tendencies.shape
    depth, height = rows.shape
    tile = 1024
    column = pl.BlockSpec((height, tile), lambda i: (0, i))
    out = pl.pallas_call(
        functools.partial(grid_kernel, scale),
        grid=(lons // tile,),
        in_specs=[
            pl.BlockSpec((depth, height), lambda i: (0, 0)),
            pl.BlockSpec((depth, tile), lambda i: (0, i)),
            column,
        ],
        out_specs=column,
        out_shape=jax.ShapeDtypeStruct((height, lons), jnp.bfloat16),
        compiler_params=pltpu.CompilerParams(vmem_limit_bytes=24 * megabyte),
        name="grid",
    )(rows, basis, tendencies.reshape(height, lons))
    return out.reshape(tendencies.shape)


def per_device(
    mem_size, ma_size, ar_state, forcing, ar_decay, amplitude, wavenumber, tables, tendencies
):
    members, waves = ar_state.shape[1], ar_state.shape[2]
    chips = mem_size // cores
    half = chips // 2
    own_table = jnp.swapaxes(tables, 1, 2)
    other_table = lax.ppermute(own_table, "mem", core_swap(mem_size))
    new_state, block = update(wavenumber, ar_decay, amplitude, ar_state, forcing)

    def shifted(value, shift):
        return lax.ppermute(value, "mem", ring_shift(mem_size, shift))

    both = (own_table, other_table)
    basis = basis_table(wavenumber, tendencies.shape[2], ma_size)
    returned = [None] * chips
    ahead = behind = block
    pending = [((block,), 0)]
    for step in range(1, half + 1):
        if step < half:
            ahead, behind = shifted(ahead, 1), shifted(behind, -1)
            arrived = [((ahead,), step), ((behind,), chips - step)]
        else:
            ahead, behind = shifted(ahead[: waves // 2], 1), shifted(behind[waves // 2 :], -1)
            arrived = [((ahead, behind), half)]
        results = legendre(both, [p for p, _ in pending], members)
        for (_, d), result in zip(pending, results):
            returned[d] = shifted(result, -d) if d else result
        pending = arrived
    results = legendre(both, [p for p, _ in pending], members)
    for (_, d), result in zip(pending, results):
        returned[d] = shifted(result, -d)
    ordered = arrange(returned)
    spread = lax.all_to_all(ordered, "ma", split_axis=0, concat_axis=0, tiled=True)
    rows = spread.reshape(-1, spread.shape[2])
    window = wavenumber.shape[0]
    perturbed = to_grid(rows, basis, tendencies, 1.0 / math.sqrt(window))
    return (perturbed, new_state)


def solution(mesh):
    return jax.shard_map(
        functools.partial(per_device, mesh.shape["mem"], mesh.shape["ma"]),
        mesh=mesh,
        in_specs=(
            P(None, "mem", "ma", None, None),
            P(None, "mem", "ma", None, None),
            P(),
            P(),
            P(),
            P("ma", None, "mem"),
            P("mem", "ma", None),
        ),
        out_specs=(P("mem", "ma", None), P(None, "mem", "ma", None, None)),
        check_vma=False,
    )
```

time: 132 us -> 85.3 us (0.65)
  starting transfers between devices: 11.7 us -> 39.3 us
  waiting for transfers between devices: 43.2 us -> 17.4 us
  local copies, waits for them, and re-layouts: 35.5 us -> 9.87 us
  other arithmetic: 19.9 us -> 0 us
  Pallas kernels: 0 us -> 17.5 us
  between operations: 14.1 us -> 0.82 us
  matrix products: 6.1 us -> 0 us
    all_gather x1 -> x0, waiting for transfers between devices: 43.2 us -> none  [per_device(): everyone = lax.all_gather(coefficients, 'mem', axis=0, tiled=True)]
    ppermute x0 -> x16, starting transfers between devices: none -> 31.9 us  [the longest x15 31.8 us: shifted(): return lax.ppermute(value, 'mem', ring_shift(mem_size, shift))]
    pallas_call x0 -> x9, Pallas kernels: none -> 17.5 us  [the longest x5 7.84 us: legendre(): pl.pallas_call(functools.partial(legendre_kernel, layout, members), in_sp...]
    ppermute x0 -> x16, waiting for transfers between devices: none -> 14.3 us  [the longest x15 14.3 us: shifted(): return lax.ppermute(value, 'mem', ring_shift(mem_size, shift))]
    another operation x2 -> x0, other arithmetic: 13.6 us -> none
    all_to_all x3 -> x0, local copies, waits for them, and re-layouts: 9.32 us -> none  [the longest x1 5.18 us: per_device(): lax.all_to_all(lax.all_to_all(fourier, 'mem', split_axis=0, concat_axis=1...]
    convert_element_type x3 -> x0, local copies, waits for them, and re-layouts: 8.13 us -> none  [the longest x1 6.47 us: basis_table(): stacked.reshape(2 * wavenumber.shape[0], lon_count).astype(jnp.bfloat16)]
    dot_general x2 -> x0, matrix products: 6.1 us -> none  [the longest x1 3.41 us: per_device(): jnp.dot(fourier_rows, basis, preferred_element_type=jnp.float32)]
  transfers between devices with their start and end apart: 3 -> 17, of which waited for: 1 -> 6; matrix products, arithmetic and copies ran while one was open for 19% -> 1% of each run, Pallas kernels for 0% -> 15%
where the time goes in v1:
time: 85.3 us; the launch traced here: 84.9 us
  starting transfers between devices  39.3 us (46%)
  Pallas kernels  17.5 us (21%)
  waiting for transfers between devices  17.4 us (20%)
  local copies, waits for them, and re-layouts  9.87 us (12%)
    ppermute x15, starting transfers between devices, shifted(): return lax.ppermute(value, 'mem', ring_shift(mem_size, shift))  31.8 us
    ppermute x15, waiting for transfers between devices, shifted(): return lax.ppermute(value, 'mem', ring_shift(mem_size, shift))  14.3 us
    unnamed x20, local copies, waits for them, and re-layouts  9.09 us
    pallas_call x5, Pallas kernels, legendre(): pl.pallas_call(functools.partial(legendre_kernel, layout, members), in_sp...  7.84 us
    all_to_all x1, starting transfers between devices, per_device(): lax.all_to_all(ordered, 'ma', split_axis=0, concat_axis=0, tiled=True)  7.48 us
    pallas_call x1, Pallas kernels, to_grid(): pl.pallas_call(functools.partial(grid_kernel, scale), grid=(lons // tile,...  4.03 us
    all_to_all x1, waiting for transfers between devices, per_device(): lax.all_to_all(ordered, 'ma', split_axis=0, concat_axis=0, tiled=True)  3.1 us
    pallas_call x1, Pallas kernels, update(): pl.pallas_call(update_kernel, grid=(waves // per_step,), in_specs=[pl.Blo...  2.92 us
  transfers between devices with their start and end apart: 17, of which 6 were waited for; matrix products, arithmetic and copies ran while one was open for 1% of the time, Pallas kernels for 15%

profile of v1, /device:TPU:2, one launch (start us, length us, event | category | flops | bytes accessed | tf_op | source)
XLA Modules:
  0.0 84.9 jit_solution(3707864859649380786)
XLA Ops:
  0.7 1.2 %copy-done.3 = f32[3,4,8,2,1280]{4,3,2,1,0:T(2,128)S(1)} copy-done((f32[3,4,8,2,1280]{4,3,2,1,0:T(2,128)S(1)}, f32[3,4,8,2,1280]{4,3,2,1,0:T(2,128)}, u32[]{:S(2)}) %copy-start.3) | copy-done | bytes 983064
  1.9 1.2 %copy-done.4 = f32[3,4,8,2,1280]{4,3,2,1,0:T(2,128)S(1)} copy-done((f32[3,4,8,2,1280]{4,3,2,1,0:T(2,128)S(1)}, f32[3,4,8,2,1280]{4,3,2,1,0:T(2,128)}, u32[]{:S(2)}) %copy-start.4) | copy-done | bytes 983064
  3.1 0.7 copy-done.5
  3.9 0.7 copy-done.6
  5.2 2.9 %update.1 = (f32[3,4,8,2,1280]{4,3,2,1,0:T(2,128)}, bf16[8,8,1280]{2,1,0:T(8,128)(2,1)S(1)}) custom-call(s32[128]{0:T(128)S(1)} %copy-done.6, f32[3]{0:T(128)S(1)} %copy-done.7, f32[3,1280]{1,0:T(4,128)S(1)} %copy-done.5, f32[3,4,8,2,1280]{4,3,2,1,0:T(2,128)S(1)} %copy-done.3, f32[3,4,8,2,1280]{4,3,2,1,0:T(2,128)S(1)} %copy-done.4), custom_call_target="tpu_custom_call" | custom-call | tf_op jit(solution)/shard_map/update/pallas_call | solution.py:58
  8.1 5.9 %collective-permute-start.2 = (bf16[8,8,1280]{2,1,0:T(8,128)(2,1)S(1)}, bf16[8,8,1280]{2,1,0:T(8,128)(2,1)S(1)}, u32[]{:S(2)}, u32[]{:S(2)}) collective-permute-start(bf16[8,8,1280]{2,1,0:T(8,128)(2,1)S(1)} %get-tuple-element.10.refs_0_), channel_id=1, source_target_pairs={{0,224},{16,240},{32,0},{48,16},{64,32},{80,48},{96,64},{112,80},{... | collective-permute-start | bytes 491528 | tf_op jit(solution)/shard_map/ppermute | solution.py:227
  14.0 4.1 %collective-permute-done.2.refs_1_ = bf16[8,8,1280]{2,1,0:T(8,128)(2,1)S(1)} collective-permute-done((bf16[8,8,1280]{2,1,0:T(8,128)(2,1)S(1)}, bf16[8,8,1280]{2,1,0:T(8,128)(2,1)S(1)}, u32[]{:S(2)}, u32[]{:S(2)}) %collective-permute-start.2) | collective-permute-done | bytes 163872 | tf_op jit(solution)/shard_map/ppermute | solution.py:227
  18.1 3.7 %collective-permute-start.5 = (bf16[8,8,1280]{2,1,0:T(8,128)(2,1)S(1)}, bf16[8,8,1280]{2,1,0:T(8,128)(2,1)S(1)}, u32[]{:S(2)}, u32[]{:S(2)}) collective-permute-start(bf16[8,8,1280]{2,1,0:T(8,128)(2,1)S(1)} %collective-permute-done.2.refs_1_), channel_id=1, source_target_pairs={{0,224},{16,240},{32,0},{48,16},{64,32},{80,48},{96,64},{112,80},{... | collective-permute-start | bytes 491528 | tf_op jit(solution)/shard_map/ppermute | solution.py:227
  21.8 3.3 %collective-permute-done.5.refs_1_ = bf16[8,8,1280]{2,1,0:T(8,128)(2,1)S(1)} collective-permute-done((bf16[8,8,1280]{2,1,0:T(8,128)(2,1)S(1)}, bf16[8,8,1280]{2,1,0:T(8,128)(2,1)S(1)}, u32[]{:S(2)}, u32[]{:S(2)}) %collective-permute-start.5) | collective-permute-done | bytes 163872 | tf_op jit(solution)/shard_map/ppermute | solution.py:227
  25.0 3.7 %collective-permute-start.8 = (bf16[8,8,1280]{2,1,0:T(8,128)(2,1)S(1)}, bf16[8,8,1280]{2,1,0:T(8,128)(2,1)S(1)}, u32[]{:S(2)}, u32[]{:S(2)}) collective-permute-start(bf16[8,8,1280]{2,1,0:T(8,128)(2,1)S(1)} %collective-permute-done.5.refs_1_), channel_id=1, source_target_pairs={{0,224},{16,240},{32,0},{48,16},{64,32},{80,48},{96,64},{112,80},{... | collective-permute-start | bytes 491528 | tf_op jit(solution)/shard_map/ppermute | solution.py:227
  28.7 0.8 copy.9.wave_ref
  29.5 2.1 %collective-permute-done.8.refs_1_ = bf16[8,8,1280]{2,1,0:T(8,128)(2,1)S(1)} collective-permute-done((bf16[8,8,1280]{2,1,0:T(8,128)(2,1)S(1)}, bf16[8,8,1280]{2,1,0:T(8,128)(2,1)S(1)}, u32[]{:S(2)}, u32[]{:S(2)}) %collective-permute-start.8) | collective-permute-done | bytes 163872 | tf_op jit(solution)/shard_map/ppermute | solution.py:227
  31.6 3.7 %collective-permute-start.11 = (bf16[4,8,1280]{2,1,0:T(8,128)(2,1)S(1)}, bf16[4,8,1280]{2,1,0:T(8,128)(2,1)S(1)}, u32[]{:S(2)}, u32[]{:S(2)}) collective-permute-start(bf16[4,8,1280]{2,1,0:T(8,128)(2,1)S(1)} %slice.9), channel_id=1, source_target_pairs={{0,224},{16,240},{32,0},{48,16},{64,32},{80,48},{96,64},{112,80},{... | collective-permute-start | bytes 245768 | tf_op jit(solution)/shard_map/ppermute | solution.py:227
  35.4 1.4 %copy-done.8 = bf16[8,1280,80]{1,2,0:T(8,128)(2,1)S(1)} copy-done((bf16[8,1280,80]{1,2,0:T(8,128)(2,1)S(1)}, bf16[8,1280,80]{1,2,0:T(8,128)(2,1)}, u32[]{:S(2)}) %copy-start.8) | copy-done | bytes 1638424
  36.8 1.9 %legendre.8 = (bf16[2,16,320]{2,1,0:T(8,128)(2,1)S(1)}, bf16[2,16,320]{2,1,0:T(8,128)(2,1)S(1)}) custom-call(bf16[8,80,1280]{2,1,0:T(8,128)(2,1)S(1)} %bitcast.9, bf16[8,80,1280]{2,1,0:T(8,128)(2,1)S(1)} %collective-permute-done.other_ref, bf16[8,8,1280]{2,1,0:T(8,128)(2,1)S(1)} %collective-permute-done.7.refs_0_, ...), custom_call_target="tpu_custom_call" | custom-call | flops 2000000000 | bytes 4194304 | tf_op jit(solution)/shard_map/legendre/pallas_call | solution.py:111
  38.8 3.8 %collective-permute-start.13 = (bf16[2,16,320]{2,1,0:T(8,128)(2,1)S(1)}, bf16[2,16,320]{2,1,0:T(8,128)(2,1)S(1)}, u32[]{:S(2)}, u32[]{:S(2)}) collective-permute-start(bf16[2,16,320]{2,1,0:T(8,128)(2,1)S(1)} %get-tuple-element.14), channel_id=1, source_target_pairs={{0,96},{16,112},{32,128},{48,144},{64,160},{80,176},{96,192},{112,... | collective-permute-start | bytes 61448 | tf_op jit(solution)/shard_map/ppermute | solution.py:227
  42.6 1.9 %legendre.7 = (bf16[2,16,320]{2,1,0:T(8,128)(2,1)S(1)}, bf16[2,16,320]{2,1,0:T(8,128)(2,1)S(1)}) custom-call(bf16[8,80,1280]{2,1,0:T(8,128)(2,1)S(1)} %bitcast.10, bf16[8,80,1280]{2,1,0:T(8,128)(2,1)S(1)} %collective-permute-done.other_ref, bf16[8,8,1280]{2,1,0:T(8,128)(2,1)S(1)} %collective-permute-done.4.refs_0_, ...), custom_call_target="tpu_custom_call" | custom-call | flops 2000000000 | bytes 4194304 | tf_op jit(solution)/shard_map/legendre/pallas_call | solution.py:111
  44.5 2.9 %collective-permute-start.6 = (bf16[2,16,320]{2,1,0:T(8,128)(2,1)S(1)}, bf16[2,16,320]{2,1,0:T(8,128)(2,1)S(1)}, u32[]{:S(2)}, u32[]{:S(2)}) collective-permute-start(bf16[2,16,320]{2,1,0:T(8,128)(2,1)S(1)} %get-tuple-element.12), channel_id=1, source_target_pairs={{0,192},{16,208},{32,224},{48,240},{64,0},{80,16},{96,32},{112,48}... | collective-permute-start | bytes 61448 | tf_op jit(solution)/shard_map/ppermute | solution.py:227
  47.5 1.9 %legendre.6 = (bf16[2,16,320]{2,1,0:T(8,128)(2,1)S(1)}, bf16[2,16,320]{2,1,0:T(8,128)(2,1)S(1)}) custom-call(bf16[8,80,1280]{2,1,0:T(8,128)(2,1)S(1)} %bitcast.11, bf16[8,80,1280]{2,1,0:T(8,128)(2,1)S(1)} %collective-permute-done.other_ref, bf16[8,8,1280]{2,1,0:T(8,128)(2,1)S(1)} %collective-permute-done.1.refs_0_, ...), custom_call_target="tpu_custom_call" | custom-call | flops 2000000000 | bytes 4194304 | tf_op jit(solution)/shard_map/legendre/pallas_call | solution.py:111
  49.7 5.6 %collective-permute-start.3 = (bf16[2,16,320]{2,1,0:T(8,128)(2,1)S(1)}, bf16[2,16,320]{2,1,0:T(8,128)(2,1)S(1)}, u32[]{:S(2)}, u32[]{:S(2)}) collective-permute-start(bf16[2,16,320]{2,1,0:T(8,128)(2,1)S(1)} %get-tuple-element.11), channel_id=1, source_target_pairs={{0,224},{16,240},{32,0},{48,16},{64,32},{80,48},{96,64},{112,80},{... | collective-permute-start | bytes 61448 | tf_op jit(solution)/shard_map/ppermute | solution.py:227
  55.4 1.1 %legendre.9 = bf16[2,16,320]{2,1,0:T(8,128)(2,1)S(1)} custom-call(bf16[8,80,1280]{2,1,0:T(8,128)(2,1)S(1)} %bitcast.12, bf16[8,80,1280]{2,1,0:T(8,128)(2,1)S(1)} %collective-permute-done.other_ref, bf16[4,8,1280]{2,1,0:T(8,128)(2,1)S(1)} %collective-permute-done.10.refs_0_, bf16[4,8,1280]{2,1,0:T(8,128)(2,1)S(1)} %collective-permute-done.11.refs_1_), custom_call_target="tpu_custom_call" | custom-call | flops 1000000000 | bytes 4194304 | tf_op jit(solution)/shard_map/legendre/pallas_call | solution.py:111
  56.5 1.9 %collective-permute-start.12 = (bf16[2,16,320]{2,1,0:T(8,128)(2,1)S(1)}, bf16[2,16,320]{2,1,0:T(8,128)(2,1)S(1)}, u32[]{:S(2)}, u32[]{:S(2)}) collective-permute-start(bf16[2,16,320]{2,1,0:T(8,128)(2,1)S(1)} %legendre.9), channel_id=1, source_target_pairs={{0,128},{16,144},{32,160},{48,176},{64,192},{80,208},{96,224},{112... | collective-permute-start | bytes 61448 | tf_op jit(solution)/shard_map/ppermute | solution.py:227
  58.4 1.1 %legendre.5.refs_0_ = bf16[2,16,320]{2,1,0:T(8,128)(2,1)S(1)} custom-call(bf16[8,80,1280]{2,1,0:T(8,128)(2,1)S(1)} %bitcast.13, bf16[8,80,1280]{2,1,0:T(8,128)(2,1)S(1)} %collective-permute-done.other_ref, bf16[8,8,1280]{2,1,0:T(8,128)(2,1)S(1)} %get-tuple-element.10.refs_0_), custom_call_target="tpu_custom_call" | custom-call | flops 1000000000 | bytes 4194304 | tf_op jit(solution)/shard_map/legendre/pallas_call | solution.py:111
  59.5 2.3 %collective-permute-done.15.refs_7_ = bf16[2,16,320]{2,1,0:T(8,128)(2,1)S(1)} collective-permute-done((bf16[2,16,320]{2,1,0:T(8,128)(2,1)S(1)}, bf16[2,16,320]{2,1,0:T(8,128)(2,1)S(1)}, u32[]{:S(2)}, u32[]{:S(2)}) %collective-permute-start.15) | collective-permute-done | bytes 20512 | tf_op jit(solution)/shard_map/ppermute | solution.py:227
  61.8 2.5 %collective-permute-done.12.refs_4_ = bf16[2,16,320]{2,1,0:T(8,128)(2,1)S(1)} collective-permute-done((bf16[2,16,320]{2,1,0:T(8,128)(2,1)S(1)}, bf16[2,16,320]{2,1,0:T(8,128)(2,1)S(1)}, u32[]{:S(2)}, u32[]{:S(2)}) %collective-permute-start.12) | collective-permute-done | bytes 20512 | tf_op jit(solution)/shard_map/ppermute | solution.py:227
  64.4 0.7 arrange.1
  65.1 7.5 %all-to-all-start = ((bf16[16,16,320]{2,1,0:T(8,128)(2,1)}), bf16[16,16,320]{2,1,0:T(8,128)(2,1)S(1)}, u32[]{:S(2)}, u32[]{:S(2)}) async-start(bf16[16,16,320]{2,1,0:T(8,128)(2,1)} %arrange.1), calls=%async_computation | async-start | bytes 393216 | tf_op jit(solution)/shard_map/all_to_all | solution.py:249
  72.6 2.0 %basis.1.basis_ref = bf16[256,5120]{1,0:T(8,128)(2,1)S(1)} custom-call(s32[128,1]{1,0:T(8,128)S(1)} %copy.9.wave_ref), custom_call_target="tpu_custom_call" | custom-call | flops 2000000000 | bytes 3145728 | tf_op jit(solution)/shard_map/basis/pallas_call | solution.py:174
  74.6 1.5 %copy-done.1 = bf16[256,5120]{1,0:T(8,128)(2,1)} copy-done((bf16[256,5120]{1,0:T(8,128)(2,1)}, bf16[256,5120]{1,0:T(8,128)(2,1)S(1)}, u32[]{:S(2)}) %copy-start.1) | copy-done | bytes 2621464
  76.0 3.1 %all-to-all-done = bf16[16,16,320]{2,1,0:T(8,128)(2,1)S(1)} async-done(((bf16[16,16,320]{2,1,0:T(8,128)(2,1)}), bf16[16,16,320]{2,1,0:T(8,128)(2,1)S(1)}, u32[]{:S(2)}, u32[]{:S(2)}) %all-to-all-start) | async-done | bytes 163872 | tf_op jit(solution)/shard_map/all_to_all | solution.py:249
  79.1 1.7 %copy-done.2 = bf16[256,5120]{1,0:T(8,128)(2,1)S(1)} copy-done((bf16[256,5120]{1,0:T(8,128)(2,1)S(1)}, bf16[256,5120]{1,0:T(8,128)(2,1)}, u32[]{:S(2)}) %copy-start.2) | copy-done | bytes 2621464
  80.9 4.0 %grid.1 = bf16[320,5120]{1,0:T(8,128)(2,1)} custom-call(bf16[256,320]{1,0:T(8,128)(2,1)S(1)} %bitcast.6, bf16[256,5120]{1,0:T(8,128)(2,1)S(1)} %copy-done.2, bf16[320,5120]{1,0:T(8,128)(2,1)S(1)} %bitcast.5), custom_call_target="tpu_custom_call" | custom-call | tf_op jit(solution)/shard_map/grid/pallas_call | solution.py:200
  (34 shorter events, 1.4 us)
Async XLA Ops:
  0.6 34.7 %collective-permute-start = (bf16[8,80,1280]{2,1,0:T(8,128)(2,1)}, bf16[8,80,1280]{2,1,0:T(8,128)(2,1)S(1)}, u32[]{:S(2)}, u32[]{:S(2)}) collective-permute-start(bf16[8,80,1280]{2,1,0:T(8,128)(2,1)} %bitcast.8), channel_id=1, source_target_pairs={{0,16},{16,0},{32,48},{48,32},{64,80},{80,64},{96,112},{112,96},{1... | collective-permute-start | bytes 4915208 | tf_op jit(solution)/shard_map/ppermute | solution.py:223
  0.7 1.2 %copy-start.3 = (f32[3,4,8,2,1280]{4,3,2,1,0:T(2,128)S(1)}, f32[3,4,8,2,1280]{4,3,2,1,0:T(2,128)}, u32[]{:S(2)}) copy-start(f32[3,4,8,2,1280]{4,3,2,1,0:T(2,128)} %state_ref.1) | copy-start | bytes 2949124
  1.9 1.2 %copy-start.4 = (f32[3,4,8,2,1280]{4,3,2,1,0:T(2,128)S(1)}, f32[3,4,8,2,1280]{4,3,2,1,0:T(2,128)}, u32[]{:S(2)}) copy-start(f32[3,4,8,2,1280]{4,3,2,1,0:T(2,128)} %forcing_ref.1) | copy-start | bytes 2949124
  3.1 0.7 copy-start.5
  3.9 0.7 copy-start.6
  4.5 0.7 copy-start.7
  8.1 10.0 %collective-permute-start.2 = (bf16[8,8,1280]{2,1,0:T(8,128)(2,1)S(1)}, bf16[8,8,1280]{2,1,0:T(8,128)(2,1)S(1)}, u32[]{:S(2)}, u32[]{:S(2)}) collective-permute-start(bf16[8,8,1280]{2,1,0:T(8,128)(2,1)S(1)} %get-tuple-element.10.refs_0_), channel_id=1, source_target_pairs={{0,224},{16,240},{32,0},{48,16},{64,32},{80,48},{96,64},{112,80},{... | collective-permute-start | bytes 491528 | tf_op jit(solution)/shard_map/ppermute | solution.py:227
  14.0 7.8 %collective-permute-start.1 = (bf16[8,8,1280]{2,1,0:T(8,128)(2,1)S(1)}, bf16[8,8,1280]{2,1,0:T(8,128)(2,1)S(1)}, u32[]{:S(2)}, u32[]{:S(2)}) collective-permute-start(bf16[8,8,1280]{2,1,0:T(8,128)(2,1)S(1)} %get-tuple-element.10.refs_0_), channel_id=1, source_target_pairs={{0,32},{16,48},{32,64},{48,80},{64,96},{80,112},{96,128},{112,144}... | collective-permute-start | bytes 491528 | tf_op jit(solution)/shard_map/ppermute | solution.py:227
  18.1 7.0 %collective-permute-start.5 = (bf16[8,8,1280]{2,1,0:T(8,128)(2,1)S(1)}, bf16[8,8,1280]{2,1,0:T(8,128)(2,1)S(1)}, u32[]{:S(2)}, u32[]{:S(2)}) collective-permute-start(bf16[8,8,1280]{2,1,0:T(8,128)(2,1)S(1)} %collective-permute-done.2.refs_1_), channel_id=1, source_target_pairs={{0,224},{16,240},{32,0},{48,16},{64,32},{80,48},{96,64},{112,80},{... | collective-permute-start | bytes 491528 | tf_op jit(solution)/shard_map/ppermute | solution.py:227
  21.8 7.0 %collective-permute-start.4 = (bf16[8,8,1280]{2,1,0:T(8,128)(2,1)S(1)}, bf16[8,8,1280]{2,1,0:T(8,128)(2,1)S(1)}, u32[]{:S(2)}, u32[]{:S(2)}) collective-permute-start(bf16[8,8,1280]{2,1,0:T(8,128)(2,1)S(1)} %collective-permute-done.1.refs_0_), channel_id=1, source_target_pairs={{0,32},{16,48},{32,64},{48,80},{64,96},{80,112},{96,128},{112,144}... | collective-permute-start | bytes 491528 | tf_op jit(solution)/shard_map/ppermute | solution.py:227
  25.0 6.5 %collective-permute-start.8 = (bf16[8,8,1280]{2,1,0:T(8,128)(2,1)S(1)}, bf16[8,8,1280]{2,1,0:T(8,128)(2,1)S(1)}, u32[]{:S(2)}, u32[]{:S(2)}) collective-permute-start(bf16[8,8,1280]{2,1,0:T(8,128)(2,1)S(1)} %collective-permute-done.5.refs_1_), channel_id=1, source_target_pairs={{0,224},{16,240},{32,0},{48,16},{64,32},{80,48},{96,64},{112,80},{... | collective-permute-start | bytes 491528 | tf_op jit(solution)/shard_map/ppermute | solution.py:227
  28.7 6.5 %collective-permute-start.7 = (bf16[8,8,1280]{2,1,0:T(8,128)(2,1)S(1)}, bf16[8,8,1280]{2,1,0:T(8,128)(2,1)S(1)}, u32[]{:S(2)}, u32[]{:S(2)}) collective-permute-start(bf16[8,8,1280]{2,1,0:T(8,128)(2,1)S(1)} %collective-permute-done.4.refs_0_), channel_id=1, source_target_pairs={{0,32},{16,48},{32,64},{48,80},{64,96},{80,112},{96,128},{112,144}... | collective-permute-start | bytes 491528 | tf_op jit(solution)/shard_map/ppermute | solution.py:227
  31.6 17.8 %collective-permute-start.11 = (bf16[4,8,1280]{2,1,0:T(8,128)(2,1)S(1)}, bf16[4,8,1280]{2,1,0:T(8,128)(2,1)S(1)}, u32[]{:S(2)}, u32[]{:S(2)}) collective-permute-start(bf16[4,8,1280]{2,1,0:T(8,128)(2,1)S(1)} %slice.9), channel_id=1, source_target_pairs={{0,224},{16,240},{32,0},{48,16},{64,32},{80,48},{96,64},{112,80},{... | collective-permute-start | bytes 245768 | tf_op jit(solution)/shard_map/ppermute | solution.py:227
  35.3 14.5 %collective-permute-start.10 = (bf16[4,8,1280]{2,1,0:T(8,128)(2,1)S(1)}, bf16[4,8,1280]{2,1,0:T(8,128)(2,1)S(1)}, u32[]{:S(2)}, u32[]{:S(2)}) collective-permute-start(bf16[4,8,1280]{2,1,0:T(8,128)(2,1)S(1)} %slice.8), channel_id=1, source_target_pairs={{0,32},{16,48},{32,64},{48,80},{64,96},{80,112},{96,128},{112,144}... | collective-permute-start | bytes 245768 | tf_op jit(solution)/shard_map/ppermute | solution.py:227
  35.4 1.4 %copy-start.8 = (bf16[8,1280,80]{1,2,0:T(8,128)(2,1)S(1)}, bf16[8,1280,80]{1,2,0:T(8,128)(2,1)}, u32[]{:S(2)}) copy-start(bf16[8,1280,80]{1,2,0:T(8,128)(2,1)} %param.12) | copy-start | bytes 4915204
  36.8 5.8 %copy-start.9 = (bf16[8,1280,80]{1,2,0:T(8,128)(2,1)S(1)}, bf16[8,1280,80]{1,2,0:T(8,128)(2,1)}, u32[]{:S(2)}) copy-start(bf16[8,1280,80]{1,2,0:T(8,128)(2,1)} %param.12) | copy-start | bytes 4915204
  38.7 17.7 %collective-permute-start.9 = (bf16[2,16,320]{2,1,0:T(8,128)(2,1)S(1)}, bf16[2,16,320]{2,1,0:T(8,128)(2,1)S(1)}, u32[]{:S(2)}, u32[]{:S(2)}) collective-permute-start(bf16[2,16,320]{2,1,0:T(8,128)(2,1)S(1)} %get-tuple-element.13), channel_id=1, source_target_pairs={{0,160},{16,176},{32,192},{48,208},{64,224},{80,240},{96,0},{112,1... | collective-permute-start | bytes 61448 | tf_op jit(solution)/shard_map/ppermute | solution.py:227
  38.8 17.7 %collective-permute-start.13 = (bf16[2,16,320]{2,1,0:T(8,128)(2,1)S(1)}, bf16[2,16,320]{2,1,0:T(8,128)(2,1)S(1)}, u32[]{:S(2)}, u32[]{:S(2)}) collective-permute-start(bf16[2,16,320]{2,1,0:T(8,128)(2,1)S(1)} %get-tuple-element.14), channel_id=1, source_target_pairs={{0,96},{16,112},{32,128},{48,144},{64,160},{80,176},{96,192},{112,... | collective-permute-start | bytes 61448 | tf_op jit(solution)/shard_map/ppermute | solution.py:227
  44.5 15.0 %collective-permute-start.6 = (bf16[2,16,320]{2,1,0:T(8,128)(2,1)S(1)}, bf16[2,16,320]{2,1,0:T(8,128)(2,1)S(1)}, u32[]{:S(2)}, u32[]{:S(2)}) collective-permute-start(bf16[2,16,320]{2,1,0:T(8,128)(2,1)S(1)} %get-tuple-element.12), channel_id=1, source_target_pairs={{0,192},{16,208},{32,224},{48,240},{64,0},{80,16},{96,32},{112,48}... | collective-permute-start | bytes 61448 | tf_op jit(solution)/shard_map/ppermute | solution.py:227
  49.4 10.1 %collective-permute-start.14 = (bf16[2,16,320]{2,1,0:T(8,128)(2,1)S(1)}, bf16[2,16,320]{2,1,0:T(8,128)(2,1)S(1)}, u32[]{:S(2)}, u32[]{:S(2)}) collective-permute-start(bf16[2,16,320]{2,1,0:T(8,128)(2,1)S(1)} %get-tuple-element.15), channel_id=1, source_target_pairs={{0,64},{16,80},{32,96},{48,112},{64,128},{80,144},{96,160},{112,17... | collective-permute-start | bytes 61448 | tf_op jit(solution)/shard_map/ppermute | solution.py:227
  49.7 9.8 %collective-permute-start.3 = (bf16[2,16,320]{2,1,0:T(8,128)(2,1)S(1)}, bf16[2,16,320]{2,1,0:T(8,128)(2,1)S(1)}, u32[]{:S(2)}, u32[]{:S(2)}) collective-permute-start(bf16[2,16,320]{2,1,0:T(8,128)(2,1)S(1)} %get-tuple-element.11), channel_id=1, source_target_pairs={{0,224},{16,240},{32,0},{48,16},{64,32},{80,48},{96,64},{112,80},{... | collective-permute-start | bytes 61448 | tf_op jit(solution)/shard_map/ppermute | solution.py:227
  56.4 5.4 %collective-permute-start.15 = (bf16[2,16,320]{2,1,0:T(8,128)(2,1)S(1)}, bf16[2,16,320]{2,1,0:T(8,128)(2,1)S(1)}, u32[]{:S(2)}, u32[]{:S(2)}) collective-permute-start(bf16[2,16,320]{2,1,0:T(8,128)(2,1)S(1)} %get-tuple-element.16), channel_id=1, source_target_pairs={{0,32},{16,48},{32,64},{48,80},{64,96},{80,112},{96,128},{112,144}... | collective-permute-start | bytes 61448 | tf_op jit(solution)/shard_map/ppermute | solution.py:227
  56.5 7.8 %collective-permute-start.12 = (bf16[2,16,320]{2,1,0:T(8,128)(2,1)S(1)}, bf16[2,16,320]{2,1,0:T(8,128)(2,1)S(1)}, u32[]{:S(2)}, u32[]{:S(2)}) collective-permute-start(bf16[2,16,320]{2,1,0:T(8,128)(2,1)S(1)} %legendre.9), channel_id=1, source_target_pairs={{0,128},{16,144},{32,160},{48,176},{64,192},{80,208},{96,224},{112... | collective-permute-start | bytes 61448 | tf_op jit(solution)/shard_map/ppermute | solution.py:227
  65.1 14.1 %all-to-all-start = ((bf16[16,16,320]{2,1,0:T(8,128)(2,1)}), bf16[16,16,320]{2,1,0:T(8,128)(2,1)S(1)}, u32[]{:S(2)}, u32[]{:S(2)}) async-start(bf16[16,16,320]{2,1,0:T(8,128)(2,1)} %arrange.1), calls=%async_computation | async-start | bytes 393216 | tf_op jit(solution)/shard_map/all_to_all | solution.py:249
  72.6 6.6 %copy-start = (bf16[4,80,5120]{2,1,0:T(8,128)(2,1)S(1)}, bf16[4,80,5120]{2,1,0:T(8,128)(2,1)}, u32[]{:S(2)}) copy-start(bf16[4,80,5120]{2,1,0:T(8,128)(2,1)} %param.13) | copy-start | bytes 9830404
  74.5 1.5 %copy-start.1 = (bf16[256,5120]{1,0:T(8,128)(2,1)}, bf16[256,5120]{1,0:T(8,128)(2,1)S(1)}, u32[]{:S(2)}) copy-start(bf16[256,5120]{1,0:T(8,128)(2,1)S(1)} %basis.1.basis_ref) | copy-start | bytes 7864324
  79.1 1.7 %copy-start.2 = (bf16[256,5120]{1,0:T(8,128)(2,1)S(1)}, bf16[256,5120]{1,0:T(8,128)(2,1)}, u32[]{:S(2)}) copy-start(bf16[256,5120]{1,0:T(8,128)(2,1)} %copy-done.1) | copy-start | bytes 7864324

commit v2 on v1

v2 whole, which is shorter than its diff:
```python
import functools
import math

import jax
import jax.numpy as jnp
from jax import lax
from jax.experimental import pallas as pl
from jax.experimental.pallas import tpu as pltpu
from jax.sharding import PartitionSpec as P

clip_level = 0.9
cores = 2
contract_last = (((1,), (1,)), ((), ()))
contract_first = (((0,), (0,)), ((), ()))
megabyte = 1 << 20


def ring_shift(mesh_size, shift):
    chips = mesh_size // cores
    return [
        (z * cores + c, ((z + shift) % chips) * cores + c) for z in range(chips) for c in range(cores)
    ]


def in_hbm(value):
    return pltpu.with_memory_space_constraint(value, pltpu.HBM)


def core_swap(mesh_size):
    return [(m, m ^ 1) for m in range(mesh_size)]


def update_kernel(
    wave_ref, decay_ref, amplitude_ref, state_hbm, forcing_hbm, new_hbm, *refs
):
    coef_refs, (state_ref, forcing_ref, new_ref, in_sems, out_sems) = refs[:2], refs[2:]
    scales, members, waves, parts, degrees = state_ref.shape
    chunks = in_sems.shape[1]
    size = waves // chunks
    loads, stores = [], []
    for i in range(chunks):
        at = (slice(None), slice(None), pl.ds(i * size, size))
        loads.append(
            [
                pltpu.make_async_copy(hbm.at[at], ref.at[at], in_sems.at[k, i])
                for k, (hbm, ref) in enumerate(((state_hbm, state_ref), (forcing_hbm, forcing_ref)))
            ]
        )
        stores.append(pltpu.make_async_copy(new_ref.at[at], new_hbm.at[at], out_sems.at[i]))
        for copy in loads[-1]:
            copy.start()
    degree = lax.broadcasted_iota(jnp.int32, (parts, degrees), 1)
    here = lax.axis_index("ma") * waves
    for i in range(chunks):
        for copy in loads[i]:
            copy.wait()
        for j in range(i * size, (i + 1) * size):
            kept = degree >= wave_ref[here + j]
            rows = []
            for b in range(members):
                total = None
                for s in range(scales):
                    value = (
                        decay_ref[s] * state_ref[s, b, j]
                        + amplitude_ref[s : s + 1, :] * forcing_ref[s, b, j]
                    )
                    value = jnp.where(kept, value, 0.0)
                    new_ref[s, b, j] = value
                    total = value if total is None else total + value
                rows.append(total)
            half = waves // len(coef_refs)
            coef_refs[j // half][j % half] = jnp.concatenate(rows, axis=0).astype(jnp.bfloat16)
        stores[i].start()
    for copy in stores:
        copy.wait()


def update(wavenumber, ar_decay, amplitude, ar_state, forcing):
    scales, members, waves, parts, degrees = ar_state.shape
    chunks, halves = 4, 2
    far = pl.BlockSpec(memory_space=pltpu.HBM)
    near = pl.BlockSpec(memory_space=pltpu.VMEM)
    coef = jax.ShapeDtypeStruct((waves // halves, members * parts, degrees), jnp.bfloat16)
    return pl.pallas_call(
        update_kernel,
        in_specs=[
            pl.BlockSpec(memory_space=pltpu.SMEM),
            pl.BlockSpec(memory_space=pltpu.SMEM),
            near,
            far,
            far,
        ],
        out_specs=[far] + [near] * halves,
        out_shape=[jax.ShapeDtypeStruct(ar_state.shape, jnp.float32)] + [coef] * halves,
        scratch_shapes=[pltpu.VMEM(ar_state.shape, jnp.float32)] * 3
        + [pltpu.SemaphoreType.DMA((2, chunks)), pltpu.SemaphoreType.DMA((chunks,))],
        compiler_params=pltpu.CompilerParams(vmem_limit_bytes=12 * megabyte),
        name="update",
    )(*(in_hbm(x) for x in (wavenumber, ar_decay, amplitude, ar_state, forcing)))


def legendre_kernel(layout, members, own_ref, other_ref, *refs):
    halves = len(layout)
    blocks, out_ref, stage = refs[:-2], refs[-2], refs[-1]
    waves, lats, _ = own_ref.shape
    chips = out_ref.shape[0]
    half = waves // halves
    core = lax.axis_index("mem") % cores
    here = lax.axis_index("mem") // cores
    rows = 2 * members
    for h, offsets in enumerate(layout):
        pieces = blocks[h * chips : (h + 1) * chips]
        for i in range(half):
            j = h * half + i
            lhs = jnp.concatenate([piece[i] for piece in pieces], axis=0)
            for side, table_ref in enumerate((own_ref, other_ref)):
                product = lax.dot_general(
                    lhs, table_ref[j], contract_last, preferred_element_type=jnp.float32
                )
                for n in range(chips):
                    for b in range(members):
                        for c in range(2):
                            r = n * rows + 2 * b + c
                            stage[n, side, c * waves + j, b * lats : (b + 1) * lats] = product[r]
    for n, offset in enumerate(layout[0]):
        there = lax.rem(here + chips - offset, chips)
        out_ref[there, core] = stage[n, 0].astype(jnp.bfloat16)
        out_ref[there, 1 - core] = stage[n, 1].astype(jnp.bfloat16)


def legendre(tables, layout, blocks, members):
    waves, lats, degrees = tables[0].shape
    chips = len(layout[0])
    whole = pl.BlockSpec(memory_space=pltpu.VMEM)
    shape = (chips, cores, 2 * waves, members * lats)
    return pl.pallas_call(
        functools.partial(legendre_kernel, layout, members),
        in_specs=[whole] * (2 + len(blocks)),
        out_specs=whole,
        out_shape=jax.ShapeDtypeStruct(shape, jnp.bfloat16),
        scratch_shapes=[pltpu.VMEM(shape, jnp.float32)],
        compiler_params=pltpu.CompilerParams(vmem_limit_bytes=8 * megabyte),
        cost_estimate=pl.CostEstimate(
            flops=4_000_000_000, bytes_accessed=4 * megabyte, transcendentals=0
        ),
        name="legendre",
    )(*tables, *blocks)


def basis_kernel(owners, wave_ref, out_ref):
    window, lanes = wave_ref.shape[0], 128
    lon_count = out_ref.shape[1]
    waves = window // owners
    tiles = lon_count // lanes
    wave = wave_ref[...]
    lane = lax.broadcasted_iota(jnp.int32, (window, lanes), 1)
    turn = 2.0 * math.pi / lon_count
    fine = (lax.rem(wave * lane, lon_count)).astype(jnp.float32) * turn
    coarse = (lax.rem(wave * lanes * lane, lon_count)).astype(jnp.float32) * turn
    cos_fine, sin_fine = jnp.cos(fine), jnp.sin(fine)
    cos_coarse, sin_coarse = jnp.cos(coarse), jnp.sin(coarse)
    for t in range(tiles):
        ca, sa = cos_coarse[:, t : t + 1], sin_coarse[:, t : t + 1]
        cosine = ca * cos_fine - sa * sin_fine
        minus_sine = -(sa * cos_fine + ca * sin_fine)
        for a in range(owners):
            rows = slice(a * waves, (a + 1) * waves)
            both = jnp.concatenate([cosine[rows], minus_sine[rows]], axis=0)
            out_ref[2 * a * waves : 2 * (a + 1) * waves, t * lanes : (t + 1) * lanes] = both.astype(
                jnp.bfloat16
            )


def basis_table(wavenumber, lon_count, owners):
    window = wavenumber.shape[0]
    return pl.pallas_call(
        functools.partial(basis_kernel, owners),
        in_specs=[pl.BlockSpec(memory_space=pltpu.VMEM)],
        out_specs=pl.BlockSpec(memory_space=pltpu.VMEM),
        out_shape=jax.ShapeDtypeStruct((2 * window, lon_count), jnp.bfloat16),
        compiler_params=pltpu.CompilerParams(vmem_limit_bytes=6 * megabyte),
        cost_estimate=pl.CostEstimate(
            flops=2_000_000_000, bytes_accessed=3 * megabyte, transcendentals=65536
        ),
        name="basis",
    )(wavenumber.reshape(window, 1))


def grid_kernel(scale, rows_ref, basis_ref, tend_ref, out_ref):
    pattern = lax.dot_general(
        rows_ref[...], basis_ref[...], contract_first, preferred_element_type=jnp.float32
    )
    pattern = jnp.clip(pattern * scale, -clip_level, clip_level)
    out_ref[...] = (tend_ref[...].astype(jnp.float32) * (1.0 + pattern)).astype(jnp.bfloat16)


def to_grid(rows, basis, tendencies, scale):
    members, lats, lons = tendencies.shape
    depth, height = rows.shape
    tile = 1024
    column = pl.BlockSpec((height, tile), lambda i: (0, i))
    out = pl.pallas_call(
        functools.partial(grid_kernel, scale),
        grid=(lons // tile,),
        in_specs=[
            pl.BlockSpec((depth, height), lambda i: (0, 0)),
            pl.BlockSpec((depth, tile), lambda i: (0, i)),
            column,
        ],
        out_specs=column,
        out_shape=jax.ShapeDtypeStruct((height, lons), jnp.bfloat16),
        compiler_params=pltpu.CompilerParams(vmem_limit_bytes=10 * megabyte),
        name="grid",
    )(rows, basis, tendencies.reshape(height, lons))
    return out.reshape(tendencies.shape)


def per_device(
    mem_size, ma_size, ar_state, forcing, ar_decay, amplitude, wavenumber, tables, tendencies
):
    members, waves = ar_state.shape[1], ar_state.shape[2]
    chips = mem_size // cores
    own_table = jnp.swapaxes(tables, 1, 2)
    other_table = lax.ppermute(own_table, "mem", core_swap(mem_size))
    other_table = pltpu.with_memory_space_constraint(other_table, pltpu.VMEM)
    new_state, *halves = update(wavenumber, ar_decay, amplitude, ar_state, forcing)
    basis = basis_table(wavenumber, tendencies.shape[2], ma_size)

    held = [{0: block} for block in halves]
    ahead, behind = list(halves), list(halves)
    for step in range(1, chips // 2 + 1):
        for h in range(2):
            if step < chips // 2 or h == 0:
                ahead[h] = lax.ppermute(ahead[h], "mem", ring_shift(mem_size, 1))
                held[h][step] = ahead[h]
            if step < chips // 2 or h == 1:
                behind[h] = lax.ppermute(behind[h], "mem", ring_shift(mem_size, -1))
                held[h][chips - step] = behind[h]
        if step == 1:
            ahead, behind, basis = lax.optimization_barrier((ahead, behind, basis))
    offsets = tuple(range(chips))
    blocks = [held[h][d] for h in range(2) for d in offsets]
    product = legendre((own_table, other_table), (offsets, offsets), blocks, members)
    groups = [[z * cores + c for z in range(chips)] for c in range(cores)]
    product = lax.all_to_all(
        product, "mem", split_axis=0, concat_axis=0, axis_index_groups=groups, tiled=True
    )
    product = product.reshape(mem_size, *product.shape[2:])
    spread = lax.all_to_all(product, "ma", split_axis=0, concat_axis=0, tiled=True)
    rows = spread.reshape(-1, spread.shape[2])
    window = wavenumber.shape[0]
    perturbed = to_grid(rows, basis, tendencies, 1.0 / math.sqrt(window))
    return (perturbed, new_state)


def solution(mesh):
    return jax.shard_map(
        functools.partial(per_device, mesh.shape["mem"], mesh.shape["ma"]),
        mesh=mesh,
        in_specs=(
            P(None, "mem", "ma", None, None),
            P(None, "mem", "ma", None, None),
            P(),
            P(),
            P(),
            P("ma", None, "mem"),
            P("mem", "ma", None),
        ),
        out_specs=(P("mem", "ma", None), P(None, "mem", "ma", None, None)),
        check_vma=False,
    )
```

time: 85.3 us -> 71.2 us (0.83)
  blocking collectives: 0 us -> 27.9 us
  starting transfers between devices: 39.3 us -> 23 us
  waiting for transfers between devices: 17.4 us -> 7.59 us
  local copies, waits for them, and re-layouts: 9.87 us -> 0.77 us
  Pallas kernels: 17.5 us -> 10.9 us
    all_to_all x0 -> x2, blocking collectives: none -> 27.9 us  [the longest x1 14.1 us: per_device(): lax.all_to_all(product, 'mem', split_axis=0, concat_axis=0, axis_index_gr...]
    unnamed x20 -> x4, local copies, waits for them, and re-layouts: 9.09 us -> 0.01 us
    ppermute x15 -> x14, starting transfers between devices: 31.8 us -> 22.9 us  [the longest x7 19.2 us: per_device(): behind[h] = lax.ppermute(behind[h], 'mem', ring_shift(mem_size, -1))]
    all_to_all x1 -> x0, starting transfers between devices: 7.48 us -> none  [per_device(): lax.all_to_all(ordered, 'ma', split_axis=0, concat_axis=0, tiled=True)]
    ppermute x15 -> x14, waiting for transfers between devices: 14.3 us -> 7.58 us  [the longest x7 7.57 us: per_device(): ahead[h] = lax.ppermute(ahead[h], 'mem', ring_shift(mem_size, 1))]
    pallas_call x5 -> x1, Pallas kernels: 7.84 us -> 1.19 us  [legendre(): pl.pallas_call(functools.partial(legendre_kernel, layout, members), in_sp...]
    all_to_all x1 -> x0, waiting for transfers between devices: 3.1 us -> none  [per_device(): lax.all_to_all(ordered, 'ma', split_axis=0, concat_axis=0, tiled=True)]
    pallas_call x2 -> x1, Pallas kernels: 3.63 us -> 3.71 us  [update(): pl.pallas_call(update_kernel, in_specs=[pl.BlockSpec(memory_space=pltpu.S...]
  transfers between devices with their start and end apart: 17 -> 15, of which waited for: 6 -> 4; matrix products, arithmetic and copies ran while one was open for 1% -> 1% of each run, Pallas kernels for 15% -> 8%
where the time goes in v2:
time: 71.2 us; the launch traced here: 70.9 us
  blocking collectives  27.9 us (39%)
  starting transfers between devices  23 us (32%)
  Pallas kernels  10.9 us (15%)
  waiting for transfers between devices  7.59 us (11%)
  local copies, waits for them, and re-layouts  0.77 us (1%)
    ppermute x7, starting transfers between devices, per_device(): behind[h] = lax.ppermute(behind[h], 'mem', ring_shift(mem_size, -1))  19.2 us
    all_to_all x1, blocking collectives, per_device(): lax.all_to_all(product, 'mem', split_axis=0, concat_axis=0, axis_index_gr...  14.1 us
    all_to_all x1, blocking collectives, per_device(): lax.all_to_all(product, 'ma', split_axis=0, concat_axis=0, tiled=True)  13.8 us
    ppermute x7, waiting for transfers between devices, per_device(): ahead[h] = lax.ppermute(ahead[h], 'mem', ring_shift(mem_size, 1))  7.57 us
    pallas_call x1, Pallas kernels, to_grid(): pl.pallas_call(functools.partial(grid_kernel, scale), grid=(lons // tile,...  4.03 us
    ppermute x7, starting transfers between devices, per_device(): ahead[h] = lax.ppermute(ahead[h], 'mem', ring_shift(mem_size, 1))  3.78 us
    pallas_call x1, Pallas kernels, update(): pl.pallas_call(update_kernel, in_specs=[pl.BlockSpec(memory_space=pltpu.S...  3.71 us
    pallas_call x1, Pallas kernels, basis_table(): pl.pallas_call(functools.partial(basis_kernel, owners), in_specs=[pl.Bloc...  1.97 us
  transfers between devices with their start and end apart: 15, of which 4 were waited for; matrix products, arithmetic and copies ran while one was open for 1% of the time, Pallas kernels for 8%

profile of v2, /device:TPU:2, one launch (start us, length us, event | category | flops | bytes accessed | tf_op | source)
XLA Modules:
  0.0 70.9 jit_solution(4565359603739721186)
XLA Ops:
  0.6 0.1 collective-permute-start
  0.7 3.7 %update.1 = (f32[3,4,8,2,1280]{4,3,2,1,0:T(2,128)}, bf16[4,8,1280]{2,1,0:T(8,128)(2,1)S(1)}, bf16[4,8,1280]{2,1,0:T(8,128)(2,1)S(1)}) custom-call(s32[128]{0:T(128)} %wave_ref.1, f32[3]{0:T(128)} %decay_ref.1, f32[3,1280]{1,0:T(4,128)} %amplitude_ref.1, f32[3,4,8,2,1280]{4,3,2,1,0:T(2,128)} %state_hbm.1, f32[3,4,8,2,1280]{4,3,2,1,0:T(2,128)} %forcing_hbm.1), custom_call_target="tpu_custom_call" | custom-call | tf_op jit(solution)/shard_map/update/pallas_call | solution.py:84
  4.5 5.9 %collective-permute-start.3 = (bf16[4,8,1280]{2,1,0:T(8,128)(2,1)S(1)}, bf16[4,8,1280]{2,1,0:T(8,128)(2,1)S(1)}, u32[]{:S(2)}, u32[]{:S(2)}) collective-permute-start(bf16[4,8,1280]{2,1,0:T(8,128)(2,1)S(1)} %get-tuple-element.10.refs_0_), channel_id=1, source_target_pairs={{0,224},{16,240},{32,0},{48,16},{64,32},{80,48},{96,64},{112,80},{... | collective-permute-start | bytes 245768 | tf_op jit(solution)/shard_map/ppermute | solution.py:237
  10.4 0.0 collective-permute-start.1
  10.4 3.2 %collective-permute-start.4 = (bf16[4,8,1280]{2,1,0:T(8,128)(2,1)S(1)}, bf16[4,8,1280]{2,1,0:T(8,128)(2,1)S(1)}, u32[]{:S(2)}, u32[]{:S(2)}) collective-permute-start(bf16[4,8,1280]{2,1,0:T(8,128)(2,1)S(1)} %get-tuple-element.11.refs_8_), channel_id=1, source_target_pairs={{0,224},{16,240},{32,0},{48,16},{64,32},{80,48},{96,64},{112,80},{... | collective-permute-start | bytes 245768 | tf_op jit(solution)/shard_map/ppermute | solution.py:237
  13.6 0.0 collective-permute-start.2
  13.6 0.8 %copy.9.wave_ref = s32[128,1]{1,0:T(8,128)S(1)} copy(s32[128,1]{0,1:T(1,128)} %bitcast.12) | data formatting | bytes 1024 | tf_op jit(solution)/shard_map/reshape | solution.py:186
  14.4 2.0 %basis.1.basis_ref = bf16[256,5120]{1,0:T(8,128)(2,1)S(1)} custom-call(s32[128,1]{1,0:T(8,128)S(1)} %copy.9.wave_ref), custom_call_target="tpu_custom_call" | custom-call | flops 2000000000 | bytes 3145728 | tf_op jit(solution)/shard_map/basis/pallas_call | solution.py:176
  16.4 0.0 collective-permute-done.3.refs_7_
  16.4 0.0 collective-permute-done.1.refs_1_
  16.4 0.0 collective-permute-done.4.refs_15_
  16.4 2.9 %collective-permute-done.2.refs_9_ = bf16[4,8,1280]{2,1,0:T(8,128)(2,1)S(1)} collective-permute-done((bf16[4,8,1280]{2,1,0:T(8,128)(2,1)S(1)}, bf16[4,8,1280]{2,1,0:T(8,128)(2,1)S(1)}, u32[]{:S(2)}, u32[]{:S(2)}) %collective-permute-start.2) | collective-permute-done | bytes 81952 | tf_op jit(solution)/shard_map/ppermute | solution.py:234
  19.3 0.0 collective-permute-start.5
  19.3 3.2 %collective-permute-start.12 = (bf16[4,8,1280]{2,1,0:T(8,128)(2,1)S(1)}, bf16[4,8,1280]{2,1,0:T(8,128)(2,1)S(1)}, u32[]{:S(2)}, u32[]{:S(2)}) collective-permute-start(bf16[4,8,1280]{2,1,0:T(8,128)(2,1)S(1)} %collective-permute-done.4.refs_15_), channel_id=1, source_target_pairs={{0,224},{16,240},{32,0},{48,16},{64,32},{80,48},{96,64},{112,80},{... | collective-permute-start | bytes 245768 | tf_op jit(solution)/shard_map/ppermute | solution.py:237
  22.5 0.0 collective-permute-start.8
  22.5 2.0 %collective-permute-start.10 = (bf16[4,8,1280]{2,1,0:T(8,128)(2,1)S(1)}, bf16[4,8,1280]{2,1,0:T(8,128)(2,1)S(1)}, u32[]{:S(2)}, u32[]{:S(2)}) collective-permute-start(bf16[4,8,1280]{2,1,0:T(8,128)(2,1)S(1)} %collective-permute-done.2.refs_9_), channel_id=1, source_target_pairs={{0,32},{16,48},{32,64},{48,80},{64,96},{80,112},{96,128},{112,144}... | collective-permute-start | bytes 245768 | tf_op jit(solution)/shard_map/ppermute | solution.py:234
  24.5 1.0 %collective-permute-done.5.refs_2_ = bf16[4,8,1280]{2,1,0:T(8,128)(2,1)S(1)} collective-permute-done((bf16[4,8,1280]{2,1,0:T(8,128)(2,1)S(1)}, bf16[4,8,1280]{2,1,0:T(8,128)(2,1)S(1)}, u32[]{:S(2)}, u32[]{:S(2)}) %collective-permute-start.5) | collective-permute-done | bytes 81952 | tf_op jit(solution)/shard_map/ppermute | solution.py:234
  25.6 3.2 %collective-permute-start.13 = (bf16[4,8,1280]{2,1,0:T(8,128)(2,1)S(1)}, bf16[4,8,1280]{2,1,0:T(8,128)(2,1)S(1)}, u32[]{:S(2)}, u32[]{:S(2)}) collective-permute-start(bf16[4,8,1280]{2,1,0:T(8,128)(2,1)S(1)} %collective-permute-done.12.refs_14_), channel_id=1, source_target_pairs={{0,224},{16,240},{32,0},{48,16},{64,32},{80,48},{96,64},{112,80},{... | collective-permute-start | bytes 245768 | tf_op jit(solution)/shard_map/ppermute | solution.py:237
  28.8 0.0 collective-permute-done.8.refs_6_
  28.8 0.3 collective-permute-start.9
  29.1 1.8 %collective-permute-start.11 = (bf16[4,8,1280]{2,1,0:T(8,128)(2,1)S(1)}, bf16[4,8,1280]{2,1,0:T(8,128)(2,1)S(1)}, u32[]{:S(2)}, u32[]{:S(2)}) collective-permute-start(bf16[4,8,1280]{2,1,0:T(8,128)(2,1)S(1)} %collective-permute-done.10.refs_10_), channel_id=1, source_target_pairs={{0,32},{16,48},{32,64},{48,80},{64,96},{80,112},{96,128},{112,144}... | collective-permute-start | bytes 245768 | tf_op jit(solution)/shard_map/ppermute | solution.py:234
  30.9 1.2 %collective-permute-done.6.refs_3_ = bf16[4,8,1280]{2,1,0:T(8,128)(2,1)S(1)} collective-permute-done((bf16[4,8,1280]{2,1,0:T(8,128)(2,1)S(1)}, bf16[4,8,1280]{2,1,0:T(8,128)(2,1)S(1)}, u32[]{:S(2)}, u32[]{:S(2)}) %collective-permute-start.6) | collective-permute-done | bytes 81952 | tf_op jit(solution)/shard_map/ppermute | solution.py:234
  32.1 0.0 collective-permute-done.13.refs_13_
  32.1 3.2 %collective-permute-start.14 = (bf16[4,8,1280]{2,1,0:T(8,128)(2,1)S(1)}, bf16[4,8,1280]{2,1,0:T(8,128)(2,1)S(1)}, u32[]{:S(2)}, u32[]{:S(2)}) collective-permute-start(bf16[4,8,1280]{2,1,0:T(8,128)(2,1)S(1)} %collective-permute-done.13.refs_13_), channel_id=1, source_target_pairs={{0,224},{16,240},{32,0},{48,16},{64,32},{80,48},{96,64},{112,80},{... | collective-permute-start | bytes 245768 | tf_op jit(solution)/shard_map/ppermute | solution.py:237
  35.3 0.0 collective-permute-done.9.refs_5_
  35.3 0.0 collective-permute-done.11.refs_11_
  35.3 2.4 %collective-permute-done.7.refs_4_ = bf16[4,8,1280]{2,1,0:T(8,128)(2,1)S(1)} collective-permute-done((bf16[4,8,1280]{2,1,0:T(8,128)(2,1)S(1)}, bf16[4,8,1280]{2,1,0:T(8,128)(2,1)S(1)}, u32[]{:S(2)}, u32[]{:S(2)}) %collective-permute-start.7) | collective-permute-done | bytes 81952 | tf_op jit(solution)/shard_map/ppermute | solution.py:234
  37.8 0.0 copy-start
  37.8 1.2 %legendre.1 = bf16[8,2,16,320]{3,2,1,0:T(8,128)(2,1)S(1)} custom-call(bf16[8,80,1280]{2,1,0:T(8,128)(2,1)S(1)} %bitcast.9, bf16[8,80,1280]{2,1,0:T(8,128)(2,1)S(1)} %collective-permute-done.other_ref, bf16[4,8,1280]{2,1,0:T(8,128)(2,1)S(1)} %get-tuple-element.10.refs_0_, bf16[4,8,1280]{2,1,0:T(8,128)(2,1)S(1)} %collective-permute-done.1.refs_1_, ...), custom_call_target="tpu_custom_call" | custom-call | flops 4000000000 | bytes 4194304 | tf_op jit(solution)/shard_map/legendre/pallas_call | solution.py:136
  39.0 14.1 %all_to_all.10 = bf16[8,2,16,320]{3,2,1,0:T(8,128)(2,1)S(1)} all-to-all(bf16[8,2,16,320]{3,2,1,0:T(8,128)(2,1)S(1)} %legendre.1), channel_id=1, replica_groups={{0,32,64,96,128,160,192,224},{16,48,80,112,144,176,208,240},{1,33,65,97..., dimensions={0} | all-to-all | bytes 327680 | tf_op jit(solution)/shard_map/all_to_all | solution.py:245
  53.1 13.8 %all_to_all.11 = bf16[16,16,320]{2,1,0:T(8,128)(2,1)S(1)} all-to-all(bf16[16,16,320]{2,1,0:T(8,128)(2,1)S(1)} %bitcast.11), channel_id=1, replica_groups=mesh['mem'=16,'ma'=16] {'ma'}, dimensions={0} | all-to-all | bytes 327680 | tf_op jit(solution)/shard_map/all_to_all | solution.py:249
  66.9 4.0 %grid.1 = bf16[320,5120]{1,0:T(8,128)(2,1)} custom-call(bf16[256,320]{1,0:T(8,128)(2,1)S(1)} %bitcast.7, bf16[256,5120]{1,0:T(8,128)(2,1)S(1)} %basis.1.basis_ref, bf16[320,5120]{1,0:T(8,128)(2,1)S(1)} %bitcast.6), custom_call_target="tpu_custom_call" | custom-call | tf_op jit(solution)/shard_map/grid/pallas_call | solution.py:202
  (9 shorter events, 0.0 us)
Async XLA Ops:
  0.6 37.1 %collective-permute-start = (bf16[8,80,1280]{2,1,0:T(8,128)(2,1)}, bf16[8,80,1280]{2,1,0:T(8,128)(2,1)S(1)}, u32[]{:S(2)}, u32[]{:S(2)}) collective-permute-start(bf16[8,80,1280]{2,1,0:T(8,128)(2,1)} %bitcast.8), channel_id=1, source_target_pairs={{0,16},{16,0},{32,48},{48,32},{64,80},{80,64},{96,112},{112,96},{1... | collective-permute-start | bytes 4915208 | tf_op jit(solution)/shard_map/ppermute | solution.py:224
  4.5 11.9 %collective-permute-start.3 = (bf16[4,8,1280]{2,1,0:T(8,128)(2,1)S(1)}, bf16[4,8,1280]{2,1,0:T(8,128)(2,1)S(1)}, u32[]{:S(2)}, u32[]{:S(2)}) collective-permute-start(bf16[4,8,1280]{2,1,0:T(8,128)(2,1)S(1)} %get-tuple-element.10.refs_0_), channel_id=1, source_target_pairs={{0,224},{16,240},{32,0},{48,16},{64,32},{80,48},{96,64},{112,80},{... | collective-permute-start | bytes 245768 | tf_op jit(solution)/shard_map/ppermute | solution.py:237
  10.4 6.0 %collective-permute-start.1 = (bf16[4,8,1280]{2,1,0:T(8,128)(2,1)S(1)}, bf16[4,8,1280]{2,1,0:T(8,128)(2,1)S(1)}, u32[]{:S(2)}, u32[]{:S(2)}) collective-permute-start(bf16[4,8,1280]{2,1,0:T(8,128)(2,1)S(1)} %get-tuple-element.10.refs_0_), channel_id=1, source_target_pairs={{0,32},{16,48},{32,64},{48,80},{64,96},{80,112},{96,128},{112,144}... | collective-permute-start | bytes 245768 | tf_op jit(solution)/shard_map/ppermute | solution.py:234
  10.4 6.0 %collective-permute-start.4 = (bf16[4,8,1280]{2,1,0:T(8,128)(2,1)S(1)}, bf16[4,8,1280]{2,1,0:T(8,128)(2,1)S(1)}, u32[]{:S(2)}, u32[]{:S(2)}) collective-permute-start(bf16[4,8,1280]{2,1,0:T(8,128)(2,1)S(1)} %get-tuple-element.11.refs_8_), channel_id=1, source_target_pairs={{0,224},{16,240},{32,0},{48,16},{64,32},{80,48},{96,64},{112,80},{... | collective-permute-start | bytes 245768 | tf_op jit(solution)/shard_map/ppermute | solution.py:237
  13.6 5.7 %collective-permute-start.2 = (bf16[4,8,1280]{2,1,0:T(8,128)(2,1)S(1)}, bf16[4,8,1280]{2,1,0:T(8,128)(2,1)S(1)}, u32[]{:S(2)}, u32[]{:S(2)}) collective-permute-start(bf16[4,8,1280]{2,1,0:T(8,128)(2,1)S(1)} %get-tuple-element.11.refs_8_), channel_id=1, source_target_pairs={{0,32},{16,48},{32,64},{48,80},{64,96},{80,112},{96,128},{112,144}... | collective-permute-start | bytes 245768 | tf_op jit(solution)/shard_map/ppermute | solution.py:234
  14.4 23.4 %copy-start.1 = (bf16[8,1280,80]{1,2,0:T(8,128)(2,1)S(1)}, bf16[8,1280,80]{1,2,0:T(8,128)(2,1)}, u32[]{:S(2)}) copy-start(bf16[8,1280,80]{1,2,0:T(8,128)(2,1)} %param.12) | copy-start | bytes 4915204
  19.3 6.3 %collective-permute-start.5 = (bf16[4,8,1280]{2,1,0:T(8,128)(2,1)S(1)}, bf16[4,8,1280]{2,1,0:T(8,128)(2,1)S(1)}, u32[]{:S(2)}, u32[]{:S(2)}) collective-permute-start(bf16[4,8,1280]{2,1,0:T(8,128)(2,1)S(1)} %collective-permute-done.1.refs_1_), channel_id=1, source_target_pairs={{0,32},{16,48},{32,64},{48,80},{64,96},{80,112},{96,128},{112,144}... | collective-permute-start | bytes 245768 | tf_op jit(solution)/shard_map/ppermute | solution.py:234
  19.3 6.3 %collective-permute-start.12 = (bf16[4,8,1280]{2,1,0:T(8,128)(2,1)S(1)}, bf16[4,8,1280]{2,1,0:T(8,128)(2,1)S(1)}, u32[]{:S(2)}, u32[]{:S(2)}) collective-permute-start(bf16[4,8,1280]{2,1,0:T(8,128)(2,1)S(1)} %collective-permute-done.4.refs_15_), channel_id=1, source_target_pairs={{0,224},{16,240},{32,0},{48,16},{64,32},{80,48},{96,64},{112,80},{... | collective-permute-start | bytes 245768 | tf_op jit(solution)/shard_map/ppermute | solution.py:237
  22.5 6.3 %collective-permute-start.8 = (bf16[4,8,1280]{2,1,0:T(8,128)(2,1)S(1)}, bf16[4,8,1280]{2,1,0:T(8,128)(2,1)S(1)}, u32[]{:S(2)}, u32[]{:S(2)}) collective-permute-start(bf16[4,8,1280]{2,1,0:T(8,128)(2,1)S(1)} %collective-permute-done.3.refs_7_), channel_id=1, source_target_pairs={{0,224},{16,240},{32,0},{48,16},{64,32},{80,48},{96,64},{112,80},{... | collective-permute-start | bytes 245768 | tf_op jit(solution)/shard_map/ppermute | solution.py:237
  22.5 6.5 %collective-permute-start.10 = (bf16[4,8,1280]{2,1,0:T(8,128)(2,1)S(1)}, bf16[4,8,1280]{2,1,0:T(8,128)(2,1)S(1)}, u32[]{:S(2)}, u32[]{:S(2)}) collective-permute-start(bf16[4,8,1280]{2,1,0:T(8,128)(2,1)S(1)} %collective-permute-done.2.refs_9_), channel_id=1, source_target_pairs={{0,32},{16,48},{32,64},{48,80},{64,96},{80,112},{96,128},{112,144}... | collective-permute-start | bytes 245768 | tf_op jit(solution)/shard_map/ppermute | solution.py:234
  25.6 6.5 %collective-permute-start.6 = (bf16[4,8,1280]{2,1,0:T(8,128)(2,1)S(1)}, bf16[4,8,1280]{2,1,0:T(8,128)(2,1)S(1)}, u32[]{:S(2)}, u32[]{:S(2)}) collective-permute-start(bf16[4,8,1280]{2,1,0:T(8,128)(2,1)S(1)} %collective-permute-done.5.refs_2_), channel_id=1, source_target_pairs={{0,32},{16,48},{32,64},{48,80},{64,96},{80,112},{96,128},{112,144}... | collective-permute-start | bytes 245768 | tf_op jit(solution)/shard_map/ppermute | solution.py:234
  25.6 6.5 %collective-permute-start.13 = (bf16[4,8,1280]{2,1,0:T(8,128)(2,1)S(1)}, bf16[4,8,1280]{2,1,0:T(8,128)(2,1)S(1)}, u32[]{:S(2)}, u32[]{:S(2)}) collective-permute-start(bf16[4,8,1280]{2,1,0:T(8,128)(2,1)S(1)} %collective-permute-done.12.refs_14_), channel_id=1, source_target_pairs={{0,224},{16,240},{32,0},{48,16},{64,32},{80,48},{96,64},{112,80},{... | collective-permute-start | bytes 245768 | tf_op jit(solution)/shard_map/ppermute | solution.py:237
  28.8 6.5 %collective-permute-start.9 = (bf16[4,8,1280]{2,1,0:T(8,128)(2,1)S(1)}, bf16[4,8,1280]{2,1,0:T(8,128)(2,1)S(1)}, u32[]{:S(2)}, u32[]{:S(2)}) collective-permute-start(bf16[4,8,1280]{2,1,0:T(8,128)(2,1)S(1)} %collective-permute-done.8.refs_6_), channel_id=1, source_target_pairs={{0,224},{16,240},{32,0},{48,16},{64,32},{80,48},{96,64},{112,80},{... | collective-permute-start | bytes 245768 | tf_op jit(solution)/shard_map/ppermute | solution.py:237
  29.1 6.3 %collective-permute-start.11 = (bf16[4,8,1280]{2,1,0:T(8,128)(2,1)S(1)}, bf16[4,8,1280]{2,1,0:T(8,128)(2,1)S(1)}, u32[]{:S(2)}, u32[]{:S(2)}) collective-permute-start(bf16[4,8,1280]{2,1,0:T(8,128)(2,1)S(1)} %collective-permute-done.10.refs_10_), channel_id=1, source_target_pairs={{0,32},{16,48},{32,64},{48,80},{64,96},{80,112},{96,128},{112,144}... | collective-permute-start | bytes 245768 | tf_op jit(solution)/shard_map/ppermute | solution.py:234
  32.1 5.7 %collective-permute-start.7 = (bf16[4,8,1280]{2,1,0:T(8,128)(2,1)S(1)}, bf16[4,8,1280]{2,1,0:T(8,128)(2,1)S(1)}, u32[]{:S(2)}, u32[]{:S(2)}) collective-permute-start(bf16[4,8,1280]{2,1,0:T(8,128)(2,1)S(1)} %collective-permute-done.6.refs_3_), channel_id=1, source_target_pairs={{0,32},{16,48},{32,64},{48,80},{64,96},{80,112},{96,128},{112,144}... | collective-permute-start | bytes 245768 | tf_op jit(solution)/shard_map/ppermute | solution.py:234
  32.1 5.6 %collective-permute-start.14 = (bf16[4,8,1280]{2,1,0:T(8,128)(2,1)S(1)}, bf16[4,8,1280]{2,1,0:T(8,128)(2,1)S(1)}, u32[]{:S(2)}, u32[]{:S(2)}) collective-permute-start(bf16[4,8,1280]{2,1,0:T(8,128)(2,1)S(1)} %collective-permute-done.13.refs_13_), channel_id=1, source_target_pairs={{0,224},{16,240},{32,0},{48,16},{64,32},{80,48},{96,64},{112,80},{... | collective-permute-start | bytes 245768 | tf_op jit(solution)/shard_map/ppermute | solution.py:237
  37.8 29.1 %copy-start = (bf16[4,80,5120]{2,1,0:T(8,128)(2,1)S(1)}, bf16[4,80,5120]{2,1,0:T(8,128)(2,1)}, u32[]{:S(2)}) copy-start(bf16[4,80,5120]{2,1,0:T(8,128)(2,1)} %param.13) | copy-start | bytes 9830404

commit v3 on v2

--- a/solution.py
+++ b/solution.py
@@ -31,12 +31,22 @@
 
 
 def update_kernel(
-    wave_ref, decay_ref, amplitude_ref, state_hbm, forcing_hbm, new_hbm, *refs
+    wave_hbm, decay_hbm, amplitude_hbm, state_hbm, forcing_hbm, new_hbm, *refs
 ):
-    coef_refs, (state_ref, forcing_ref, new_ref, in_sems, out_sems) = refs[:2], refs[2:]
+    coef_refs, refs = refs[:2], refs[2:]
+    wave_ref, decay_ref, amplitude_ref, state_ref, forcing_ref, new_ref = refs[:6]
+    small_sems, in_sems, out_sems = refs[6:]
     scales, members, waves, parts, degrees = state_ref.shape
     chunks = in_sems.shape[1]
     size = waves // chunks
+    small = [
+        pltpu.make_async_copy(hbm, ref, small_sems.at[k])
+        for k, (hbm, ref) in enumerate(
+            ((wave_hbm, wave_ref), (decay_hbm, decay_ref), (amplitude_hbm, amplitude_ref))
+        )
+    ]
+    for copy in small:
+        copy.start()
     loads, stores = [], []
     for i in range(chunks):
         at = (slice(None), slice(None), pl.ds(i * size, size))
@@ -51,6 +61,12 @@
             copy.start()
     degree = lax.broadcasted_iota(jnp.int32, (parts, degrees), 1)
     here = lax.axis_index("ma") * waves
+    for copy in small:
+        copy.wait()
+    decay = [decay_ref[s] for s in range(scales)]
+    amplitude = [
+        jnp.broadcast_to(amplitude_ref[s : s + 1, :], (parts, degrees)) for s in range(scales)
+    ]
     for i in range(chunks):
         for copy in loads[i]:
             copy.wait()
@@ -60,10 +76,7 @@
             for b in range(members):
                 total = None
                 for s in range(scales):
-                    value = (
-                        decay_ref[s] * state_ref[s, b, j]
-                        + amplitude_ref[s : s + 1, :] * forcing_ref[s, b, j]
-                    )
+                    value = decay[s] * state_ref[s, b, j] + amplitude[s] * forcing_ref[s, b, j]
                     value = jnp.where(kept, value, 0.0)
                     new_ref[s, b, j] = value
                     total = value if total is None else total + value
@@ -83,17 +96,20 @@
     coef = jax.ShapeDtypeStruct((waves // halves, members * parts, degrees), jnp.bfloat16)
     return pl.pallas_call(
         update_kernel,
-        in_specs=[
-            pl.BlockSpec(memory_space=pltpu.SMEM),
-            pl.BlockSpec(memory_space=pltpu.SMEM),
-            near,
-            far,
-            far,
-        ],
+        in_specs=[far] * 5,
         out_specs=[far] + [near] * halves,
         out_shape=[jax.ShapeDtypeStruct(ar_state.shape, jnp.float32)] + [coef] * halves,
-        scratch_shapes=[pltpu.VMEM(ar_state.shape, jnp.float32)] * 3
-        + [pltpu.SemaphoreType.DMA((2, chunks)), pltpu.SemaphoreType.DMA((chunks,))],
+        scratch_shapes=[
+            pltpu.SMEM(wavenumber.shape, jnp.int32),
+            pltpu.SMEM(ar_decay.shape, jnp.float32),
+            pltpu.VMEM(amplitude.shape, jnp.float32),
+        ]
+        + [pltpu.VMEM(ar_state.shape, jnp.float32)] * 3
+        + [
+            pltpu.SemaphoreType.DMA((3,)),
+            pltpu.SemaphoreType.DMA((2, chunks)),
+            pltpu.SemaphoreType.DMA((chunks,)),
+        ],
         compiler_params=pltpu.CompilerParams(vmem_limit_bytes=12 * megabyte),
         name="update",
     )(*(in_hbm(x) for x in (wavenumber, ar_decay, amplitude, ar_state, forcing)))
@@ -148,11 +164,11 @@
 
 
 def basis_kernel(owners, wave_ref, out_ref):
-    window, lanes = wave_ref.shape[0], 128
+    window, lanes = wave_ref.shape[1], 128
     lon_count = out_ref.shape[1]
     waves = window // owners
     tiles = lon_count // lanes
-    wave = wave_ref[...]
+    wave = jnp.transpose(jnp.broadcast_to(wave_ref[...], (lanes, window)))
     lane = lax.broadcasted_iota(jnp.int32, (window, lanes), 1)
     turn = 2.0 * math.pi / lon_count
     fine = (lax.rem(wave * lane, lon_count)).astype(jnp.float32) * turn
@@ -183,33 +199,41 @@
             flops=2_000_000_000, bytes_accessed=3 * megabyte, transcendentals=65536
         ),
         name="basis",
-    )(wavenumber.reshape(window, 1))
-
-
-def grid_kernel(scale, rows_ref, basis_ref, tend_ref, out_ref):
-    pattern = lax.dot_general(
-        rows_ref[...], basis_ref[...], contract_first, preferred_element_type=jnp.float32
-    )
-    pattern = jnp.clip(pattern * scale, -clip_level, clip_level)
-    out_ref[...] = (tend_ref[...].astype(jnp.float32) * (1.0 + pattern)).astype(jnp.bfloat16)
+    )(wavenumber.reshape(1, window))
+
+
+def grid_kernel(scale, rows_ref, basis_ref, tend_ref, out_hbm, stage, sems):
+    height, lons = stage.shape
+    tiles = sems.shape[0]
+    tile = lons // tiles
+    rows = jnp.transpose(rows_ref[...].astype(jnp.float32)).astype(jnp.bfloat16)
+    copies = []
+    for i in range(tiles):
+        at = (slice(None), pl.ds(i * tile, tile))
+        pattern = jnp.dot(rows, basis_ref[at], preferred_element_type=jnp.float32)
+        pattern = jnp.clip(pattern * scale, -clip_level, clip_level)
+        stage[at] = (tend_ref[at].astype(jnp.float32) * (1.0 + pattern)).astype(jnp.bfloat16)
+        copies.append(pltpu.make_async_copy(stage.at[at], out_hbm.at[at], sems.at[i]))
+        copies[-1].start()
+    for copy in copies:
+        copy.wait()
 
 
 def to_grid(rows, basis, tendencies, scale):
     members, lats, lons = tendencies.shape
-    depth, height = rows.shape
-    tile = 1024
-    column = pl.BlockSpec((height, tile), lambda i: (0, i))
+    height = rows.shape[1]
+    tiles = 10
+    near = pl.BlockSpec(memory_space=pltpu.VMEM)
     out = pl.pallas_call(
         functools.partial(grid_kernel, scale),
-        grid=(lons // tile,),
-        in_specs=[
-            pl.BlockSpec((depth, height), lambda i: (0, 0)),
-            pl.BlockSpec((depth, tile), lambda i: (0, i)),
-            column,
+        in_specs=[near] * 3,
+        out_specs=pl.BlockSpec(memory_space=pltpu.HBM),
+        out_shape=jax.ShapeDtypeStruct((height, lons), jnp.bfloat16),
+        scratch_shapes=[
+            pltpu.VMEM((height, lons), jnp.bfloat16),
+            pltpu.SemaphoreType.DMA((tiles,)),
         ],
-        out_specs=column,
-        out_shape=jax.ShapeDtypeStruct((height, lons), jnp.bfloat16),
-        compiler_params=pltpu.CompilerParams(vmem_limit_bytes=10 * megabyte),
+        compiler_params=pltpu.CompilerParams(vmem_limit_bytes=12 * megabyte),
         name="grid",
     )(rows, basis, tendencies.reshape(height, lons))
     return out.reshape(tendencies.shape)
@@ -224,20 +248,22 @@
     other_table = lax.ppermute(own_table, "mem", core_swap(mem_size))
     other_table = pltpu.with_memory_space_constraint(other_table, pltpu.VMEM)
     new_state, *halves = update(wavenumber, ar_decay, amplitude, ar_state, forcing)
-    basis = basis_table(wavenumber, tendencies.shape[2], ma_size)
+
+    def shifted(value, shift):
+        return lax.ppermute(value, "mem", ring_shift(mem_size, shift))
 
     held = [{0: block} for block in halves]
-    ahead, behind = list(halves), list(halves)
-    for step in range(1, chips // 2 + 1):
-        for h in range(2):
-            if step < chips // 2 or h == 0:
-                ahead[h] = lax.ppermute(ahead[h], "mem", ring_shift(mem_size, 1))
-                held[h][step] = ahead[h]
-            if step < chips // 2 or h == 1:
-                behind[h] = lax.ppermute(behind[h], "mem", ring_shift(mem_size, -1))
-                held[h][chips - step] = behind[h]
-        if step == 1:
-            ahead, behind, basis = lax.optimization_barrier((ahead, behind, basis))
+    furthest = chips // 2
+    for step in range(1, furthest):
+        for h, way in ((0, 1), (1, -1), (1, 1), (0, -1)):
+            last = held[h][way * (step - 1) % chips]
+            if step == furthest - 1 and h == (way < 0):
+                held[h][furthest] = shifted(last, 2 * way)
+            held[h][way * step % chips] = shifted(last, way)
+    late, timed = lax.optimization_barrier((held[0][chips - 2], wavenumber))
+    held[0][chips - 2] = late
+    basis = basis_table(timed, tendencies.shape[2], ma_size)
+    held[1][furthest], basis = lax.optimization_barrier((held[1][furthest], basis))
     offsets = tuple(range(chips))
     blocks = [held[h][d] for h in range(2) for d in offsets]
     product = legendre((own_table, other_table), (offsets, offsets), blocks, members)

time: 71.2 us -> 65.3 us (0.917)
  waiting for transfers between devices: 7.59 us -> 5.1 us
  Pallas kernels: 10.9 us -> 8.98 us
  blocking collectives: 27.9 us -> 26 us
    ppermute x14, waiting for transfers between devices: 7.58 us -> 5.09 us  [shifted(): return lax.ppermute(value, 'mem', ring_shift(mem_size, shift))]
    pallas_call x2, Pallas kernels: 7.75 us -> 5.83 us  [the longest x1 3.33 us: update(): pl.pallas_call(update_kernel, in_specs=[far] * 5, out_specs=[far] + [near...]
    all_to_all x1, blocking collectives: 14.1 us -> 12.2 us  [per_device(): lax.all_to_all(product, 'mem', split_axis=0, concat_axis=0, axis_index_gr...]
    reshape x1 -> x0, local copies, waits for them, and re-layouts: 0.76 us -> none  [basis_table(): wavenumber.reshape(window, 1)]
  transfers between devices with their start and end apart: 15 -> 15, of which waited for: 4 -> 5; matrix products, arithmetic and copies ran while one was open for 1% -> 0% of each run, Pallas kernels for 8% -> 8%
where the time goes in v3:
time: 65.3 us; the launch traced here: 65.1 us
  blocking collectives  26 us (40%)
  starting transfers between devices  23.5 us (36%)
  Pallas kernels  8.98 us (14%)
  waiting for transfers between devices  5.1 us (8%)
  between operations  0.85 us (1%)
  local copies, waits for them, and re-layouts  0.66 us (1%)
    ppermute x14, starting transfers between devices, shifted(): return lax.ppermute(value, 'mem', ring_shift(mem_size, shift))  23.4 us
    all_to_all x1, blocking collectives, per_device(): lax.all_to_all(product, 'ma', split_axis=0, concat_axis=0, tiled=True)  13.8 us
    all_to_all x1, blocking collectives, per_device(): lax.all_to_all(product, 'mem', split_axis=0, concat_axis=0, axis_index_gr...  12.2 us
    ppermute x14, waiting for transfers between devices, shifted(): return lax.ppermute(value, 'mem', ring_shift(mem_size, shift))  5.09 us
    pallas_call x1, Pallas kernels, update(): pl.pallas_call(update_kernel, in_specs=[far] * 5, out_specs=[far] + [near...  3.33 us
    pallas_call x1, Pallas kernels, to_grid(): pl.pallas_call(functools.partial(grid_kernel, scale), in_specs=[near] * 3...  2.5 us
    pallas_call x1, Pallas kernels, basis_table(): pl.pallas_call(functools.partial(basis_kernel, owners), in_specs=[pl.Bloc...  1.96 us
  transfers between devices with their start and end apart: 15, of which 5 were waited for; matrix products, arithmetic and copies ran while one was open for 0% of the time, Pallas kernels for 8%

profile of v3, /device:TPU:2, one launch (start us, length us, event | category | flops | bytes accessed | tf_op | source)
XLA Modules:
  0.0 65.1 jit_solution(6518598646272387547)
XLA Ops:
  0.6 0.1 collective-permute-start
  0.7 3.3 %update.1 = (f32[3,4,8,2,1280]{4,3,2,1,0:T(2,128)}, bf16[4,8,1280]{2,1,0:T(8,128)(2,1)S(1)}, bf16[4,8,1280]{2,1,0:T(8,128)(2,1)S(1)}) custom-call(s32[128]{0:T(128)} %wave_hbm.1, f32[3]{0:T(128)} %decay_hbm.1, f32[3,1280]{1,0:T(4,128)} %amplitude_hbm.1, f32[3,4,8,2,1280]{4,3,2,1,0:T(2,128)} %state_hbm.1, f32[3,4,8,2,1280]{4,3,2,1,0:T(2,128)} %forcing_hbm.1), custom_call_target="tpu_custom_call" | custom-call | tf_op jit(solution)/shard_map/update/pallas_call | solution.py:97
  4.1 5.9 %collective-permute-start.5 = (bf16[4,8,1280]{2,1,0:T(8,128)(2,1)S(1)}, bf16[4,8,1280]{2,1,0:T(8,128)(2,1)S(1)}, u32[]{:S(2)}, u32[]{:S(2)}) collective-permute-start(bf16[4,8,1280]{2,1,0:T(8,128)(2,1)S(1)} %get-tuple-element.9.refs_0_), channel_id=1, source_target_pairs={{0,224},{16,240},{32,0},{48,16},{64,32},{80,48},{96,64},{112,80},{... | collective-permute-start | bytes 245768 | tf_op jit(solution)/shard_map/ppermute | solution.py:253
  10.0 1.0 %collective-permute-start.11 = (bf16[4,8,1280]{2,1,0:T(8,128)(2,1)S(1)}, bf16[4,8,1280]{2,1,0:T(8,128)(2,1)S(1)}, u32[]{:S(2)}, u32[]{:S(2)}) collective-permute-start(bf16[4,8,1280]{2,1,0:T(8,128)(2,1)S(1)} %get-tuple-element.11.refs_8_), channel_id=1, source_target_pairs={{0,224},{16,240},{32,0},{48,16},{64,32},{80,48},{96,64},{112,80},{... | collective-permute-start | bytes 245768 | tf_op jit(solution)/shard_map/ppermute | solution.py:253
  11.0 1.0 %collective-permute-start.1 = (bf16[4,8,1280]{2,1,0:T(8,128)(2,1)S(1)}, bf16[4,8,1280]{2,1,0:T(8,128)(2,1)S(1)}, u32[]{:S(2)}, u32[]{:S(2)}) collective-permute-start(bf16[4,8,1280]{2,1,0:T(8,128)(2,1)S(1)} %get-tuple-element.9.refs_0_), channel_id=1, source_target_pairs={{0,32},{16,48},{32,64},{48,80},{64,96},{80,112},{96,128},{112,144}... | collective-permute-start | bytes 245768 | tf_op jit(solution)/shard_map/ppermute | solution.py:253
  12.0 0.0 collective-permute-start.8
  12.1 0.8 %collective-permute-done.5.refs_7_ = bf16[4,8,1280]{2,1,0:T(8,128)(2,1)S(1)} collective-permute-done((bf16[4,8,1280]{2,1,0:T(8,128)(2,1)S(1)}, bf16[4,8,1280]{2,1,0:T(8,128)(2,1)S(1)}, u32[]{:S(2)}, u32[]{:S(2)}) %collective-permute-start.5) | collective-permute-done | bytes 81952 | tf_op jit(solution)/shard_map/ppermute | solution.py:253
  12.8 3.7 %collective-permute-start.6 = (bf16[4,8,1280]{2,1,0:T(8,128)(2,1)S(1)}, bf16[4,8,1280]{2,1,0:T(8,128)(2,1)S(1)}, u32[]{:S(2)}, u32[]{:S(2)}) collective-permute-start(bf16[4,8,1280]{2,1,0:T(8,128)(2,1)S(1)} %collective-permute-done.5.refs_7_), channel_id=1, source_target_pairs={{0,224},{16,240},{32,0},{48,16},{64,32},{80,48},{96,64},{112,80},{... | collective-permute-start | bytes 245768 | tf_op jit(solution)/shard_map/ppermute | solution.py:253
  16.5 0.0 collective-permute-done.11.refs_15_
  16.5 1.3 %collective-permute-start.12 = (bf16[4,8,1280]{2,1,0:T(8,128)(2,1)S(1)}, bf16[4,8,1280]{2,1,0:T(8,128)(2,1)S(1)}, u32[]{:S(2)}, u32[]{:S(2)}) collective-permute-start(bf16[4,8,1280]{2,1,0:T(8,128)(2,1)S(1)} %collective-permute-done.11.refs_15_), channel_id=1, source_target_pairs={{0,224},{16,240},{32,0},{48,16},{64,32},{80,48},{96,64},{112,80},{... | collective-permute-start | bytes 245768 | tf_op jit(solution)/shard_map/ppermute | solution.py:253
  17.8 0.7 %collective-permute-start.2 = (bf16[4,8,1280]{2,1,0:T(8,128)(2,1)S(1)}, bf16[4,8,1280]{2,1,0:T(8,128)(2,1)S(1)}, u32[]{:S(2)}, u32[]{:S(2)}) collective-permute-start(bf16[4,8,1280]{2,1,0:T(8,128)(2,1)S(1)} %collective-permute-done.1.refs_1_), channel_id=1, source_target_pairs={{0,32},{16,48},{32,64},{48,80},{64,96},{80,112},{96,128},{112,144}... | collective-permute-start | bytes 245768 | tf_op jit(solution)/shard_map/ppermute | solution.py:253
  18.6 0.1 collective-permute-start.9
  18.6 0.7 %collective-permute-done.6.refs_6_ = bf16[4,8,1280]{2,1,0:T(8,128)(2,1)S(1)} collective-permute-done((bf16[4,8,1280]{2,1,0:T(8,128)(2,1)S(1)}, bf16[4,8,1280]{2,1,0:T(8,128)(2,1)S(1)}, u32[]{:S(2)}, u32[]{:S(2)}) %collective-permute-start.6) | collective-permute-done | bytes 81952 | tf_op jit(solution)/shard_map/ppermute | solution.py:253
  19.3 3.7 %collective-permute-start.7 = (bf16[4,8,1280]{2,1,0:T(8,128)(2,1)S(1)}, bf16[4,8,1280]{2,1,0:T(8,128)(2,1)S(1)}, u32[]{:S(2)}, u32[]{:S(2)}) collective-permute-start(bf16[4,8,1280]{2,1,0:T(8,128)(2,1)S(1)} %collective-permute-done.6.refs_6_), channel_id=1, source_target_pairs={{0,224},{16,240},{32,0},{48,16},{64,32},{80,48},{96,64},{112,80},{... | collective-permute-start | bytes 245768 | tf_op jit(solution)/shard_map/ppermute | solution.py:253
  23.0 0.0 collective-permute-start.13
  23.0 0.6 collective-permute-done.2.refs_2_
  23.6 2.3 %collective-permute-start.4 = (bf16[4,8,1280]{2,1,0:T(8,128)(2,1)S(1)}, bf16[4,8,1280]{2,1,0:T(8,128)(2,1)S(1)}, u32[]{:S(2)}, u32[]{:S(2)}) collective-permute-start(bf16[4,8,1280]{2,1,0:T(8,128)(2,1)S(1)} %collective-permute-done.2.refs_2_), channel_id=1, source_target_pairs={{0,64},{16,80},{32,96},{48,112},{64,128},{80,144},{96,160},{112,17... | collective-permute-start | bytes 245768 | tf_op jit(solution)/shard_map/ppermute | solution.py:253
  25.9 0.0 collective-permute-done.9.refs_10_
  25.9 0.0 collective-permute-start.3
  26.0 0.0 collective-permute-done.7.refs_5_
  26.0 3.6 %collective-permute-start.14 = (bf16[4,8,1280]{2,1,0:T(8,128)(2,1)S(1)}, bf16[4,8,1280]{2,1,0:T(8,128)(2,1)S(1)}, u32[]{:S(2)}, u32[]{:S(2)}) collective-permute-start(bf16[4,8,1280]{2,1,0:T(8,128)(2,1)S(1)} %collective-permute-done.12.refs_14_), channel_id=1, source_target_pairs={{0,224},{16,240},{32,0},{48,16},{64,32},{80,48},{96,64},{112,80},{... | collective-permute-start | bytes 245768 | tf_op jit(solution)/shard_map/ppermute | solution.py:253
  29.5 0.0 collective-permute-done.13.refs_12_
  29.5 0.0 collective-permute-start.10
  29.5 0.7 %copy-done.1 = s32[128]{0:T(128)S(1)} copy-done((s32[128]{0:T(128)S(1)}, s32[128]{0:T(128)}, u32[]{:S(2)}) %copy-start.1) | copy-done | bytes 536
  30.2 2.0 %basis.1.basis_ref = bf16[256,5120]{1,0:T(8,128)(2,1)S(1)} custom-call(s32[1,128]{1,0:T(1,128)S(1)} %bitcast.8), custom_call_target="tpu_custom_call" | custom-call | flops 2000000000 | bytes 3145728 | tf_op jit(solution)/shard_map/basis/pallas_call | solution.py:192
  32.2 0.0 collective-permute-done.4.refs_4_
  32.2 0.9 %collective-permute-done.3.refs_3_ = bf16[4,8,1280]{2,1,0:T(8,128)(2,1)S(1)} collective-permute-done((bf16[4,8,1280]{2,1,0:T(8,128)(2,1)S(1)}, bf16[4,8,1280]{2,1,0:T(8,128)(2,1)S(1)}, u32[]{:S(2)}, u32[]{:S(2)}) %collective-permute-start.3) | collective-permute-done | bytes 81952 | tf_op jit(solution)/shard_map/ppermute | solution.py:253
  33.1 2.1 %collective-permute-done.10.refs_11_ = bf16[4,8,1280]{2,1,0:T(8,128)(2,1)S(1)} collective-permute-done((bf16[4,8,1280]{2,1,0:T(8,128)(2,1)S(1)}, bf16[4,8,1280]{2,1,0:T(8,128)(2,1)S(1)}, u32[]{:S(2)}, u32[]{:S(2)}) %collective-permute-start.10) | collective-permute-done | bytes 81952 | tf_op jit(solution)/shard_map/ppermute | solution.py:253
  35.2 1.2 %legendre.1 = bf16[8,2,16,320]{3,2,1,0:T(8,128)(2,1)S(1)} custom-call(bf16[8,80,1280]{2,1,0:T(8,128)(2,1)S(1)} %bitcast.10, bf16[8,80,1280]{2,1,0:T(8,128)(2,1)S(1)} %collective-permute-done.other_ref, bf16[4,8,1280]{2,1,0:T(8,128)(2,1)S(1)} %get-tuple-element.9.refs_0_, bf16[4,8,1280]{2,1,0:T(8,128)(2,1)S(1)} %collective-permute-done.1.refs_1_, ...), custom_call_target="tpu_custom_call" | custom-call | flops 4000000000 | bytes 4194304 | tf_op jit(solution)/shard_map/legendre/pallas_call | solution.py:152
  36.4 12.2 %all_to_all.10 = bf16[8,2,16,320]{3,2,1,0:T(8,128)(2,1)S(1)} all-to-all(bf16[8,2,16,320]{3,2,1,0:T(8,128)(2,1)S(1)} %legendre.1), channel_id=1, replica_groups={{0,32,64,96,128,160,192,224},{16,48,80,112,144,176,208,240},{1,33,65,97..., dimensions={0} | all-to-all | bytes 327680 | tf_op jit(solution)/shard_map/all_to_all | solution.py:271
  48.6 13.8 %all_to_all.11 = bf16[16,16,320]{2,1,0:T(8,128)(2,1)S(1)} all-to-all(bf16[16,16,320]{2,1,0:T(8,128)(2,1)S(1)} %bitcast.12), channel_id=1, replica_groups=mesh['mem'=16,'ma'=16] {'ma'}, dimensions={0} | all-to-all | bytes 327680 | tf_op jit(solution)/shard_map/all_to_all | solution.py:275
  62.4 2.5 %grid.1 = bf16[320,5120]{1,0:T(8,128)(2,1)} custom-call(bf16[256,320]{1,0:T(8,128)(2,1)S(1)} %bitcast.7, bf16[256,5120]{1,0:T(8,128)(2,1)S(1)} %basis.1.basis_ref, bf16[320,5120]{1,0:T(8,128)(2,1)S(1)} %bitcast.6), custom_call_target="tpu_custom_call" | custom-call | tf_op jit(solution)/shard_map/grid/pallas_call | solution.py:227
  (10 shorter events, 0.0 us)
Async XLA Ops:
  0.6 34.6 %collective-permute-start = (bf16[8,80,1280]{2,1,0:T(8,128)(2,1)}, bf16[8,80,1280]{2,1,0:T(8,128)(2,1)S(1)}, u32[]{:S(2)}, u32[]{:S(2)}) collective-permute-start(bf16[8,80,1280]{2,1,0:T(8,128)(2,1)} %bitcast.9), channel_id=1, source_target_pairs={{0,16},{16,0},{32,48},{48,32},{64,80},{80,64},{96,112},{112,96},{1... | collective-permute-start | bytes 4915208 | tf_op jit(solution)/shard_map/ppermute | solution.py:248
  4.1 8.8 %collective-permute-start.5 = (bf16[4,8,1280]{2,1,0:T(8,128)(2,1)S(1)}, bf16[4,8,1280]{2,1,0:T(8,128)(2,1)S(1)}, u32[]{:S(2)}, u32[]{:S(2)}) collective-permute-start(bf16[4,8,1280]{2,1,0:T(8,128)(2,1)S(1)} %get-tuple-element.9.refs_0_), channel_id=1, source_target_pairs={{0,224},{16,240},{32,0},{48,16},{64,32},{80,48},{96,64},{112,80},{... | collective-permute-start | bytes 245768 | tf_op jit(solution)/shard_map/ppermute | solution.py:253
  10.0 6.5 %collective-permute-start.11 = (bf16[4,8,1280]{2,1,0:T(8,128)(2,1)S(1)}, bf16[4,8,1280]{2,1,0:T(8,128)(2,1)S(1)}, u32[]{:S(2)}, u32[]{:S(2)}) collective-permute-start(bf16[4,8,1280]{2,1,0:T(8,128)(2,1)S(1)} %get-tuple-element.11.refs_8_), channel_id=1, source_target_pairs={{0,224},{16,240},{32,0},{48,16},{64,32},{80,48},{96,64},{112,80},{... | collective-permute-start | bytes 245768 | tf_op jit(solution)/shard_map/ppermute | solution.py:253
  11.0 6.8 %collective-permute-start.1 = (bf16[4,8,1280]{2,1,0:T(8,128)(2,1)S(1)}, bf16[4,8,1280]{2,1,0:T(8,128)(2,1)S(1)}, u32[]{:S(2)}, u32[]{:S(2)}) collective-permute-start(bf16[4,8,1280]{2,1,0:T(8,128)(2,1)S(1)} %get-tuple-element.9.refs_0_), channel_id=1, source_target_pairs={{0,32},{16,48},{32,64},{48,80},{64,96},{80,112},{96,128},{112,144}... | collective-permute-start | bytes 245768 | tf_op jit(solution)/shard_map/ppermute | solution.py:253
  12.0 6.5 %collective-permute-start.8 = (bf16[4,8,1280]{2,1,0:T(8,128)(2,1)S(1)}, bf16[4,8,1280]{2,1,0:T(8,128)(2,1)S(1)}, u32[]{:S(2)}, u32[]{:S(2)}) collective-permute-start(bf16[4,8,1280]{2,1,0:T(8,128)(2,1)S(1)} %get-tuple-element.11.refs_8_), channel_id=1, source_target_pairs={{0,32},{16,48},{32,64},{48,80},{64,96},{80,112},{96,128},{112,144}... | collective-permute-start | bytes 245768 | tf_op jit(solution)/shard_map/ppermute | solution.py:253
  12.8 6.5 %collective-permute-start.6 = (bf16[4,8,1280]{2,1,0:T(8,128)(2,1)S(1)}, bf16[4,8,1280]{2,1,0:T(8,128)(2,1)S(1)}, u32[]{:S(2)}, u32[]{:S(2)}) collective-permute-start(bf16[4,8,1280]{2,1,0:T(8,128)(2,1)S(1)} %collective-permute-done.5.refs_7_), channel_id=1, source_target_pairs={{0,224},{16,240},{32,0},{48,16},{64,32},{80,48},{96,64},{112,80},{... | collective-permute-start | bytes 245768 | tf_op jit(solution)/shard_map/ppermute | solution.py:253
  16.5 6.5 %collective-permute-start.12 = (bf16[4,8,1280]{2,1,0:T(8,128)(2,1)S(1)}, bf16[4,8,1280]{2,1,0:T(8,128)(2,1)S(1)}, u32[]{:S(2)}, u32[]{:S(2)}) collective-permute-start(bf16[4,8,1280]{2,1,0:T(8,128)(2,1)S(1)} %collective-permute-done.11.refs_15_), channel_id=1, source_target_pairs={{0,224},{16,240},{32,0},{48,16},{64,32},{80,48},{96,64},{112,80},{... | collective-permute-start | bytes 245768 | tf_op jit(solution)/shard_map/ppermute | solution.py:253
  17.8 5.8 %collective-permute-start.2 = (bf16[4,8,1280]{2,1,0:T(8,128)(2,1)S(1)}, bf16[4,8,1280]{2,1,0:T(8,128)(2,1)S(1)}, u32[]{:S(2)}, u32[]{:S(2)}) collective-permute-start(bf16[4,8,1280]{2,1,0:T(8,128)(2,1)S(1)} %collective-permute-done.1.refs_1_), channel_id=1, source_target_pairs={{0,32},{16,48},{32,64},{48,80},{64,96},{80,112},{96,128},{112,144}... | collective-permute-start | bytes 245768 | tf_op jit(solution)/shard_map/ppermute | solution.py:253
  18.6 7.4 %collective-permute-start.9 = (bf16[4,8,1280]{2,1,0:T(8,128)(2,1)S(1)}, bf16[4,8,1280]{2,1,0:T(8,128)(2,1)S(1)}, u32[]{:S(2)}, u32[]{:S(2)}) collective-permute-start(bf16[4,8,1280]{2,1,0:T(8,128)(2,1)S(1)} %collective-permute-done.8.refs_9_), channel_id=1, source_target_pairs={{0,32},{16,48},{32,64},{48,80},{64,96},{80,112},{96,128},{112,144}... | collective-permute-start | bytes 245768 | tf_op jit(solution)/shard_map/ppermute | solution.py:253
  19.3 6.6 %collective-permute-start.7 = (bf16[4,8,1280]{2,1,0:T(8,128)(2,1)S(1)}, bf16[4,8,1280]{2,1,0:T(8,128)(2,1)S(1)}, u32[]{:S(2)}, u32[]{:S(2)}) collective-permute-start(bf16[4,8,1280]{2,1,0:T(8,128)(2,1)S(1)} %collective-permute-done.6.refs_6_), channel_id=1, source_target_pairs={{0,224},{16,240},{32,0},{48,16},{64,32},{80,48},{96,64},{112,80},{... | collective-permute-start | bytes 245768 | tf_op jit(solution)/shard_map/ppermute | solution.py:253
  23.0 6.5 %collective-permute-start.13 = (bf16[4,8,1280]{2,1,0:T(8,128)(2,1)S(1)}, bf16[4,8,1280]{2,1,0:T(8,128)(2,1)S(1)}, u32[]{:S(2)}, u32[]{:S(2)}) collective-permute-start(bf16[4,8,1280]{2,1,0:T(8,128)(2,1)S(1)} %collective-permute-done.12.refs_14_), channel_id=1, source_target_pairs={{0,192},{16,208},{32,224},{48,240},{64,0},{80,16},{96,32},{112,48}... | collective-permute-start | bytes 245768 | tf_op jit(solution)/shard_map/ppermute | solution.py:253
  23.6 8.6 %collective-permute-start.4 = (bf16[4,8,1280]{2,1,0:T(8,128)(2,1)S(1)}, bf16[4,8,1280]{2,1,0:T(8,128)(2,1)S(1)}, u32[]{:S(2)}, u32[]{:S(2)}) collective-permute-start(bf16[4,8,1280]{2,1,0:T(8,128)(2,1)S(1)} %collective-permute-done.2.refs_2_), channel_id=1, source_target_pairs={{0,64},{16,80},{32,96},{48,112},{64,128},{80,144},{96,160},{112,17... | collective-permute-start | bytes 245768 | tf_op jit(solution)/shard_map/ppermute | solution.py:253
  25.9 7.2 %collective-permute-start.3 = (bf16[4,8,1280]{2,1,0:T(8,128)(2,1)S(1)}, bf16[4,8,1280]{2,1,0:T(8,128)(2,1)S(1)}, u32[]{:S(2)}, u32[]{:S(2)}) collective-permute-start(bf16[4,8,1280]{2,1,0:T(8,128)(2,1)S(1)} %collective-permute-done.2.refs_2_), channel_id=1, source_target_pairs={{0,32},{16,48},{32,64},{48,80},{64,96},{80,112},{96,128},{112,144}... | collective-permute-start | bytes 245768 | tf_op jit(solution)/shard_map/ppermute | solution.py:253
  26.0 7.2 %collective-permute-start.14 = (bf16[4,8,1280]{2,1,0:T(8,128)(2,1)S(1)}, bf16[4,8,1280]{2,1,0:T(8,128)(2,1)S(1)}, u32[]{:S(2)}, u32[]{:S(2)}) collective-permute-start(bf16[4,8,1280]{2,1,0:T(8,128)(2,1)S(1)} %collective-permute-done.12.refs_14_), channel_id=1, source_target_pairs={{0,224},{16,240},{32,0},{48,16},{64,32},{80,48},{96,64},{112,80},{... | collective-permute-start | bytes 245768 | tf_op jit(solution)/shard_map/ppermute | solution.py:253
  29.5 5.7 %collective-permute-start.10 = (bf16[4,8,1280]{2,1,0:T(8,128)(2,1)S(1)}, bf16[4,8,1280]{2,1,0:T(8,128)(2,1)S(1)}, u32[]{:S(2)}, u32[]{:S(2)}) collective-permute-start(bf16[4,8,1280]{2,1,0:T(8,128)(2,1)S(1)} %collective-permute-done.9.refs_10_), channel_id=1, source_target_pairs={{0,32},{16,48},{32,64},{48,80},{64,96},{80,112},{96,128},{112,144}... | collective-permute-start | bytes 245768 | tf_op jit(solution)/shard_map/ppermute | solution.py:253
  29.5 0.7 %copy-start.1 = (s32[128]{0:T(128)S(1)}, s32[128]{0:T(128)}, u32[]{:S(2)}) copy-start(s32[128]{0:T(128)} %wave_hbm.1) | copy-start | bytes 1540
  30.2 5.0 %copy-start.2 = (bf16[8,1280,80]{1,2,0:T(8,128)(2,1)S(1)}, bf16[8,1280,80]{1,2,0:T(8,128)(2,1)}, u32[]{:S(2)}) copy-start(bf16[8,1280,80]{1,2,0:T(8,128)(2,1)} %param.12) | copy-start | bytes 4915204
  35.2 27.2 %copy-start = (bf16[4,80,5120]{2,1,0:T(8,128)(2,1)S(1)}, bf16[4,80,5120]{2,1,0:T(8,128)(2,1)}, u32[]{:S(2)}) copy-start(bf16[4,80,5120]{2,1,0:T(8,128)(2,1)} %param.13) | copy-start | bytes 9830404
